TPU v7x, 16 devices: a 4x2x1 block of a 4x4x8 slice. The times are simulated.
16 devices in a mesh: dp: 2 (over y, z), tp: 8 (over x, core).
Axes of the slice: x: 4, y: 2, z: 1, core: 2. Of those that a mesh axis runs over, the one named last changes fastest.
The devices are a block of a 4x4x8 slice.
Arguments:
- x_in: bfloat16 [32, 512, 1024], P('dp', 'tp'), parts along dimension 0
- grad_y: bfloat16 [32, 512, 1024], P('dp', 'tp'), parts along dimension 0
- pad_mask: int32 [32, 512], P('dp'), parts along dimension 0
- ln1_gain: float32 [1024], replicated
- ln1_bias: float32 [1024], replicated
- w_qkv: bfloat16 [3, 1024, 16, 64], P(None, None, 'tp')
- b_qkv: float32 [3, 16, 64], P(None, 'tp')
- w_out: bfloat16 [16, 64, 1024], P('tp')
- b_out: float32 [1024], replicated
- ln2_gain: float32 [1024], replicated
- ln2_bias: float32 [1024], replicated
- w_up: bfloat16 [1024, 4096], P(None, 'tp')
- b_up: float32 [4096], P('tp')
- w_down: bfloat16 [4096, 1024], P('tp')
- b_down: float32 [1024], replicated
Outputs:
- output 1: bfloat16 [32, 512, 1024], P('dp', 'tp'), parts along dimension 0
- output 2: bfloat16 [32, 512, 1024], P('dp', 'tp'), parts along dimension 0
- output 3: float32 [2048], P('dp'), parts along dimension 0
- output 4: float32 [2048], P('dp'), parts along dimension 0
- output 5: float32 [6, 1024, 16, 64], P('dp', None, 'tp'), parts along dimension 0
- output 6: float32 [6, 16, 64], P('dp', 'tp'), parts along dimension 0
- output 7: float32 [32, 64, 1024], P(('dp', 'tp')), parts along dimension 0
- output 8: float32 [2048], P('dp'), parts along dimension 0
- output 9: float32 [2048], P('dp'), parts along dimension 0
- output 10: float32 [2048], P('dp'), parts along dimension 0
- output 11: float32 [2048, 4096], P('dp', 'tp'), parts along dimension 0
- output 12: float32 [8192], P(('dp', 'tp')), parts along dimension 0
- output 13: float32 [8192, 1024], P(('dp', 'tp')), parts along dimension 0
- output 14: float32 [2048], P('dp'), parts along dimension 0
There are 2 independent parts. A program takes and returns all parts, laid end to end along the dimension named above; an argument that names none is the same for every part.
All inputs are finite; a program needn't handle non-finite values.
Results may differ from a plain program's by a relative error of at most 0.0122089.
Values are sent between devices in bfloat16 or wider.
A program may use at most 768 MiB of HBM per device.

v0:
```python
import jax
import jax.numpy as jnp
from jax import lax
from jax.sharding import PartitionSpec as P

LN_EPS = 1e-5
ROPE_BASE = 10000.0
INV_SQRT2 = 0.7071067811865476
INV_SQRT_2PI = 0.3989422804014327
NEG_LARGE = -1e30


def layer_norm(values, ln_gain, ln_bias):
    centered = values - jnp.mean(values, axis=-1, keepdims=True)
    inv_std = lax.rsqrt(jnp.mean(centered * centered, axis=-1, keepdims=True) + LN_EPS)
    x_hat = centered * inv_std
    return x_hat * ln_gain + ln_bias, x_hat, inv_std


def layer_norm_grad(d_out, x_hat, inv_std, ln_gain):
    d_hat = d_out * ln_gain
    return inv_std * (d_hat - jnp.mean(d_hat, axis=-1, keepdims=True) - x_hat * jnp.mean(d_hat * x_hat, axis=-1, keepdims=True))


def rope_tables(seq_len, head_dim):
    half_dim = head_dim // 2
    inv_freq = ROPE_BASE ** (-2.0 * jnp.arange(half_dim, dtype=jnp.float32) / head_dim)
    angles = jnp.arange(seq_len, dtype=jnp.float32)[:, None] * inv_freq[None, :]
    angles = jnp.concatenate([angles, angles], axis=-1)
    return jnp.cos(angles)[:, None, :], jnp.sin(angles)[:, None, :]


def rotate(tensor, cos_tab, sin_tab):
    half_dim = tensor.shape[-1] // 2
    swapped = jnp.concatenate([-tensor[..., half_dim:], tensor[..., :half_dim]], axis=-1)
    return tensor * cos_tab + swapped * sin_tab


def rotate_back(grad_in, cos_tab, sin_tab):
    half_dim = grad_in.shape[-1] // 2
    scaled = grad_in * sin_tab
    swapped = jnp.concatenate([scaled[..., half_dim:], -scaled[..., :half_dim]], axis=-1)
    return grad_in * cos_tab + swapped


def solution(mesh):
    act_spec = P('dp', 'tp', None)
    rep_vec = P(None)
    part_vec = P('dp')
    in_specs = (act_spec, act_spec, P('dp', None), rep_vec, rep_vec, P(None, None, 'tp', None), P(None, 'tp', None),
                P('tp', None, None), rep_vec, rep_vec, rep_vec, P(None, 'tp'), P('tp'), P('tp', None), rep_vec)
    out_specs = (act_spec, act_spec, part_vec, part_vec, P('dp', None, 'tp', None), P('dp', 'tp', None),
                 P(('dp', 'tp'), None, None), part_vec, part_vec, part_vec, P('dp', 'tp'), P(('dp', 'tp')),
                 P(('dp', 'tp'), None), part_vec)

    def device_step(x_in, grad_y, pad_mask, ln1_gain, ln1_bias, w_qkv, b_qkv, w_out, b_out, ln2_gain, ln2_bias, w_up, b_up, w_down, b_down):
        seq_len = pad_mask.shape[1]
        head_dim = w_qkv.shape[3]
        q_scale = head_dim ** -0.5
        cos_tab, sin_tab = rope_tables(seq_len, head_dim)
        key_ok = (pad_mask > 0)[:, None, None, :]
        x_f = x_in.astype(jnp.float32)
        h1_f, x_hat1, inv_std1 = layer_norm(x_f, ln1_gain, ln1_bias)
        h1_full = lax.all_gather(h1_f.astype(jnp.bfloat16), 'tp', axis=1, tiled=True)
        qkv_all = jnp.einsum('bsd,idhk->ibshk', h1_full, w_qkv, preferred_element_type=jnp.float32) + b_qkv[:, None, None]
        q_rot = rotate(qkv_all[0] * q_scale, cos_tab, sin_tab).astype(jnp.bfloat16)
        k_rot = rotate(qkv_all[1], cos_tab, sin_tab).astype(jnp.bfloat16)
        v_heads = qkv_all[2].astype(jnp.bfloat16)
        scores = jnp.einsum('bqhk,bshk->bhqs', q_rot, k_rot, preferred_element_type=jnp.float32)
        attn_probs = jax.nn.softmax(jnp.where(key_ok, scores, NEG_LARGE), axis=-1)
        probs_low = attn_probs.astype(jnp.bfloat16)
        attn_o = jnp.einsum('bhqs,bshk->bqhk', probs_low, v_heads, preferred_element_type=jnp.float32).astype(jnp.bfloat16)
        attn_part = jnp.einsum('cril,ile->cre', attn_o, w_out, preferred_element_type=jnp.float32)
        attn_sum = lax.psum_scatter(attn_part, 'tp', scatter_dimension=1, tiled=True)
        x1_f = (x_f + (attn_sum + b_out)).astype(jnp.bfloat16).astype(jnp.float32)
        h2_f, x_hat2, inv_std2 = layer_norm(x1_f, ln2_gain, ln2_bias)
        h2_full = lax.all_gather(h2_f.astype(jnp.bfloat16), 'tp', axis=1, tiled=True)
        pre_act = jnp.einsum('bsd,df->bsf', h2_full, w_up, preferred_element_type=jnp.float32) + b_up
        erf_term = lax.erf(pre_act * INV_SQRT2)
        act_b = (0.5 * pre_act * (1.0 + erf_term)).astype(jnp.bfloat16)
        gelu_slope = 0.5 * (1.0 + erf_term) + pre_act * jnp.exp(-0.5 * pre_act * pre_act) * INV_SQRT_2PI
        mlp_part = jnp.einsum('bsf,fd->bsd', act_b, w_down, preferred_element_type=jnp.float32)
        mlp_sum = lax.psum_scatter(mlp_part, 'tp', scatter_dimension=1, tiled=True)
        y_out = (x1_f + (mlp_sum + b_down)).astype(jnp.bfloat16)
        dy_full = lax.all_gather(grad_y, 'tp', axis=1, tiled=True)
        dy_f = grad_y.astype(jnp.float32)
        grad_w_down = jnp.einsum('bsf,bsd->fd', act_b, dy_full, preferred_element_type=jnp.float32)
        d_act = jnp.einsum('bsd,fd->bsf', dy_full, w_down, preferred_element_type=jnp.float32)
        d_pre = d_act * gelu_slope
        grad_b_up = jnp.sum(d_pre, axis=(0, 1))
        d_pre_b = d_pre.astype(jnp.bfloat16)
        grad_w_up = jnp.einsum('bsd,bsf->df', h2_full, d_pre_b, preferred_element_type=jnp.float32)
        d_h2_part = jnp.einsum('bsf,df->bsd', d_pre_b, w_up, preferred_element_type=jnp.float32)
        d_h2 = lax.psum_scatter(d_h2_part, 'tp', scatter_dimension=1, tiled=True)
        d_x1 = dy_f + layer_norm_grad(d_h2, x_hat2, inv_std2, ln2_gain)
        mid_sums = lax.psum(jnp.stack([jnp.sum(dy_f, axis=(0, 1)), jnp.sum(d_h2 * x_hat2, axis=(0, 1)),
                                       jnp.sum(d_h2, axis=(0, 1)), jnp.sum(d_x1, axis=(0, 1))]), 'tp')
        d_x1_full = lax.all_gather(d_x1.astype(jnp.bfloat16), 'tp', axis=1, tiled=True)
        grad_w_out = jnp.einsum('bshk,bsd->hkd', attn_o, d_x1_full, preferred_element_type=jnp.float32)
        d_attn_o = jnp.einsum('bsd,hkd->bshk', d_x1_full, w_out, preferred_element_type=jnp.float32).astype(jnp.bfloat16)
        d_value = jnp.einsum('bhqs,bqhk->bshk', probs_low, d_attn_o, preferred_element_type=jnp.float32)
        d_probs = jnp.einsum('bqhk,bshk->bhqs', d_attn_o, v_heads, preferred_element_type=jnp.float32)
        d_scores = (attn_probs * (d_probs - jnp.sum(d_probs * attn_probs, axis=-1, keepdims=True))).astype(jnp.bfloat16)
        d_query = jnp.einsum('bhqs,bshk->bqhk', d_scores, k_rot, preferred_element_type=jnp.float32)
        d_key = jnp.einsum('bhqs,bqhk->bshk', d_scores, q_rot, preferred_element_type=jnp.float32)
        d_qkv = jnp.stack([rotate_back(d_query, cos_tab, sin_tab) * q_scale, rotate_back(d_key, cos_tab, sin_tab), d_value])
        grad_b_qkv = jnp.sum(d_qkv, axis=(1, 2))
        d_qkv_b = d_qkv.astype(jnp.bfloat16)
        grad_w_qkv = jnp.einsum('bsd,ibshk->idhk', h1_full, d_qkv_b, preferred_element_type=jnp.float32)
        d_h1_part = jnp.einsum('ibshk,idhk->bsd', d_qkv_b, w_qkv, preferred_element_type=jnp.float32)
        d_h1 = lax.psum_scatter(d_h1_part, 'tp', scatter_dimension=1, tiled=True)
        ln1_sums = lax.psum(jnp.stack([jnp.sum(d_h1 * x_hat1, axis=(0, 1)), jnp.sum(d_h1, axis=(0, 1))]), 'tp')
        grad_x = (d_x1 + layer_norm_grad(d_h1, x_hat1, inv_std1, ln1_gain)).astype(jnp.bfloat16)
        return (y_out, grad_x, ln1_sums[0], ln1_sums[1], grad_w_qkv, grad_b_qkv, grad_w_out, mid_sums[3],
                mid_sums[1], mid_sums[2], grad_w_up, grad_b_up, grad_w_down, mid_sums[0])

    return jax.shard_map(device_step, mesh=mesh, in_specs=in_specs, out_specs=out_specs, check_vma=False)
```

profile of v0, /device:TPU:113, one launch (start us, length us, event | category | flops | bytes accessed | tf_op | source)
XLA Modules:
  0.0 1312.8 jit_solution(7578963256901412174)
XLA Ops:
  15.8 83.3 %all-gather.5.cloned.1.call-done = bf16[16,512,1024]{2,1,0:T(8,128)(2,1)} async-done(((bf16[16,64,1024]{2,1,0:T(8,128)(2,1)}), bf16[16,512,1024]{2,1,0:T(8,128)(2,1)}) %all-gather.5.cloned.1.call-update) | async-done | bytes 16777232 | tf_op jit(solution)/shard_map/all_gather | solution.py:64
  126.0 16.6 %fusion.134 = (f32[16,2,512]{2,1,0:T(2,128)S(1)}, f32[16,2,512,512]{2,3,1,0:T(8,128)}) fusion(pred[16,512]{1,0:T(8,128)(4,1)S(1)} %broadcast_compare_fusion, bf16[16,512,2,64]{1,3,2,0:T(8,128)(2,1)} %get-tuple-element.29, bf16[16,512,2,64]{1,3,2,0:T(8,128)(2,1)} %get-tuple-element.28), kind=kOutput, calls=%fused_computation.147 | convolution fusion | flops 1098908160 | bytes 37822464 | tf_op jit(solution)/shard_map/sub | solution.py:70
  142.6 17.0 %fusion.80 = bf16[16,2,64,512]{3,2,1,0:T(8,128)(2,1)} fusion(f32[3,16,512,2,64]{2,4,3,0,1:T(8,128)} %copy-done.8, f32[16,2,512]{2,1,0:T(2,128)S(1)} %get-tuple-element.53, pred[16,512]{1,0:T(8,128)(4,1)S(1)} %broadcast_compare_fusion, bf16[16,512,2,64]{1,3,2,0:T(8,128)(2,1)} %get-tuple-element.29, bf16[16,512,2,64]{1,3,2,0:T(8,128)(2,1)} %get-tuple-element.28), kind=kOutput, calls=%fused_computation.108 | convolution fusion | flops 2182103552 | bytes 8462336 | tf_op jit(solution)/shard_map/bhqs,bshk->bqhk/dot_general | solution.py:72
  159.6 14.8 %convolution_bitcast_fusion.1 = f32[16,512,1024]{2,1,0:T(8,128)} fusion(bf16[16,2,64,512]{3,2,1,0:T(8,128)(2,1)} %fusion.80, bf16[2,64,1024]{2,1,0:T(8,128)(2,1)S(1)} %copy-done.14), kind=kOutput, calls=%fused_computation.26 | convolution fusion | flops 2147483648 | bytes 35913728 | tf_op jit(solution)/shard_map/cril,ile->cre/dot_general | solution.py:73
  174.6 166.2 %reduce-scatter.5.cloned.1.call-done = f32[16,64,1024]{2,1,0:T(8,128)} async-done(((f32[16,512,1024]{2,1,0:T(8,128)}), f32[16,64,1024]{2,1,0:T(8,128)}) %reduce-scatter.5.cloned.1.call-update) | async-done | bytes 4194320 | tf_op jit(solution)/shard_map/reduce_scatter | solution.py:74
  347.9 81.0 %all-gather.7.cloned.1.call-done = bf16[16,512,1024]{2,1,0:T(8,128)(2,1)} async-done(((bf16[16,64,1024]{2,1,0:T(8,128)(2,1)}), bf16[16,512,1024]{2,1,0:T(8,128)(2,1)}) %all-gather.7.cloned.1.call-update) | async-done | bytes 16777232 | tf_op jit(solution)/shard_map/all_gather | solution.py:77
  428.9 20.0 %multiply_convert_fusion.1 = (bf16[16,512,512]{2,1,0:T(8,128)(2,1)}, f32[16,512,512]{2,1,0:T(8,128)}) fusion(f32[512]{0:T(512)S(1)} %copy-done.34, bf16[16,512,1024]{2,1,0:T(8,128)(2,1)} %all-gather.7.cloned.1.call-done, bf16[1024,512]{1,0:T(8,128)(2,1)S(1)} %copy-done), kind=kOutput, calls=%fused_computation.20 | convolution fusion | flops 8615100416 | bytes 42993664 | tf_op jit(solution)/shard_map/bsd,df->bsf/dot_general | solution.py:78
  448.9 63.1 %all-gather.9.cloned.1.call-done = bf16[16,512,1024]{2,1,0:T(8,128)(2,1)} async-done(((bf16[16,64,1024]{2,1,0:T(8,128)(2,1)}), bf16[16,512,1024]{2,1,0:T(8,128)(2,1)}) %all-gather.9.cloned.1.call-update) | async-done | bytes 16777232 | tf_op jit(solution)/shard_map/all_gather | solution.py:85
  512.0 21.6 %fusion.135 = (f32[512]{0:T(512)}, bf16[16,512,512]{2,1,0:T(8,128)(2,1)}) fusion(f32[16,512,512]{2,1,0:T(8,128)} %get-tuple-element.56, f32[512]{0:T(512)S(1)} %copy-done.34, bf16[16,512,1024]{2,1,0:T(8,128)(2,1)} %all-gather.9.cloned.1.call-done, bf16[512,1024]{1,0:T(8,128)(2,1)S(1)} %copy-done.31), kind=kOutput, calls=%fused_computation.148 | convolution fusion | flops 8640266240 | bytes 42995712 | tf_op jit(solution)/shard_map/bsd,fd->bsf/dot_general | solution.py:88
  533.6 18.9 %fusion.66 = f32[16,512,1024]{2,1,0:T(8,128)} fusion(bf16[16,512,512]{2,1,0:T(8,128)(2,1)} %get-tuple-element.61, bf16[1024,512]{1,0:T(8,128)(2,1)S(1)} %copy-done), kind=kOutput, calls=%fused_computation.94 | convolution fusion | flops 8589934592 | bytes 42991616 | tf_op jit(solution)/shard_map/bsf,df->bsd/dot_general | solution.py:93
  552.7 18.7 %fusion.95 = f32[16,512,1024]{2,1,0:T(8,128)} fusion(bf16[16,512,512]{2,1,0:T(8,128)(2,1)} %get-tuple-element.55, bf16[512,1024]{1,0:T(8,128)(2,1)S(1)} %copy-done.31), kind=kOutput, calls=%fused_computation.114 | convolution fusion | flops 8589934592 | bytes 42991616 | tf_op jit(solution)/shard_map/bsf,fd->bsd/dot_general | solution.py:82
  571.6 147.3 %reduce-scatter.9.cloned.1.call-done = f32[16,64,1024]{2,1,0:T(8,128)} async-done(((f32[16,512,1024]{2,1,0:T(8,128)}), f32[16,64,1024]{2,1,0:T(8,128)}) %reduce-scatter.9.cloned.1.call-update) | async-done | bytes 4194320 | tf_op jit(solution)/shard_map/reduce_scatter | solution.py:94
  723.1 164.1 %reduce-scatter.7.cloned.1.call-done = f32[16,64,1024]{2,1,0:T(8,128)} async-done(((f32[16,512,1024]{2,1,0:T(8,128)}), f32[16,64,1024]{2,1,0:T(8,128)}) %reduce-scatter.7.cloned.1.call-update) | async-done | bytes 4194320 | tf_op jit(solution)/shard_map/reduce_scatter | solution.py:83
  898.3 17.6 %fusion.184 = bf16[16,2,512,512]{2,3,1,0:T(8,128)(2,1)} fusion(f32[16,2,512]{2,1,0:T(2,128)S(1)} %get-tuple-element.53, pred[16,512]{1,0:T(8,128)(4,1)S(1)} %broadcast_compare_fusion, bf16[16,512,2,64]{1,3,2,0:T(8,128)(2,1)S(1)} %copy-done.9, bf16[16,512,2,64]{1,3,2,0:T(8,128)(2,1)} %get-tuple-element.28), kind=kOutput, calls=%fused_computation.32.clone.clone.clone.1 | convolution fusion | flops 1107313152 | bytes 21045248 | tf_op jit(solution)/shard_map/sub | solution.py:70
  915.8 63.6 %all-gather.11.cloned.1.call-done = bf16[16,512,1024]{2,1,0:T(8,128)(2,1)} async-done(((bf16[16,64,1024]{2,1,0:T(8,128)(2,1)}), bf16[16,512,1024]{2,1,0:T(8,128)(2,1)}) %all-gather.11.cloned.1.call-update) | async-done | bytes 16777232 | tf_op jit(solution)/shard_map/all_gather | solution.py:98
  992.1 13.6 %fusion.71 = f32[1,16,512,2,64]{2,4,3,1,0:T(8,128)} fusion(bf16[16,512,2,64]{1,3,2,0:T(8,128)(2,1)} %fusion.77, bf16[16,2,512,512]{2,3,1,0:T(8,128)(2,1)} %fusion.184), kind=kOutput, calls=%fused_computation.99 | convolution fusion | flops 1073741824 | bytes 23068672 | tf_op jit(solution)/shard_map/bhqs,bqhk->bshk/dot_general | solution.py:101
  1005.7 23.3 %multiply_reduce_fusion = (f32[16,2,512]{2,1,0:T(2,128)S(1)}, f32[16,2,512,512]{2,3,1,0:T(8,128)}) fusion(f32[16,2,512,512]{2,3,1,0:T(8,128)} %get-tuple-element.54, f32[16,2,512]{2,1,0:T(2,128)S(1)} %get-tuple-element.53, bf16[16,512,2,64]{1,3,2,0:T(8,128)(2,1)} %fusion.77, f32[3,16,512,2,64]{2,4,3,0,1:T(8,128)} %copy-done.8), kind=kOutput, calls=%fused_computation.2 | convolution fusion | flops 1098891264 | bytes 71434240 | tf_op jit(solution)/shard_map/bqhk,bshk->bhqs/dot_general | solution.py:102
  1029.0 27.6 %multiply_convert_fusion = bf16[16,2,512,512]{2,3,1,0:T(8,128)(2,1)} fusion(f32[16,2,512,512]{2,3,1,0:T(8,128)} %get-tuple-element.58, f32[16,2,512]{2,1,0:T(2,128)S(1)} %get-tuple-element.57, f32[16,2,512,512]{2,3,1,0:T(8,128)} %get-tuple-element.54, f32[16,2,512]{2,1,0:T(2,128)S(1)} %get-tuple-element.53), kind=kLoop, calls=%fused_computation.1 | loop fusion | flops 33554432 | bytes 84017152 | tf_op jit(solution)/shard_map/convert_element_type | solution.py:103
  1087.2 20.3 %convolution_bitcast_fusion = f32[16,512,1024]{2,1,0:T(8,128)} fusion(bf16[3,1024,2,64]{1,3,2,0:T(8,128)(2,1)S(1)} %copy-done.32, f32[1,16,512,2,64]{2,4,3,1,0:T(8,128)} %fusion.71, f32[1,16,512,2,64]{2,4,3,1,0:T(8,128)} %get-tuple-element.41, f32[1,16,512,2,64]{2,4,3,1,0:T(8,128)} %get-tuple-element.40), kind=kOutput, calls=%fused_computation.25 | convolution fusion | flops 6448742400 | bytes 46923776 | tf_op jit(solution)/shard_map/ibshk,idhk->bsd/dot_general | solution.py:110
  1107.5 15.9 %convolution_bitcast_fusion.2 = f32[512,1024]{1,0:T(8,128)} fusion(bf16[16,512,512]{2,1,0:T(8,128)(2,1)} %get-tuple-element.55, bf16[16,512,1024]{2,1,0:T(8,128)(2,1)} %all-gather.9.cloned.1.call-done), kind=kOutput, calls=%fused_computation.110 | convolution fusion | flops 8589934592 | bytes 27262976 | tf_op jit(solution)/shard_map/bsf,bsd->fd/dot_general | solution.py:87
  1123.5 16.1 %fusion.83 = f32[1024,512]{1,0:T(8,128)} fusion(bf16[16,512,1024]{2,1,0:T(8,128)(2,1)} %all-gather.7.cloned.1.call-done, bf16[16,512,512]{2,1,0:T(8,128)(2,1)} %get-tuple-element.61), kind=kOutput, calls=%fused_computation.109 | convolution fusion | flops 8589934592 | bytes 27262976 | tf_op jit(solution)/shard_map/bsd,bsf->df/dot_general | solution.py:92
  1150.3 15.5 %fusion.86 = f32[3,1024,2,64]{1,3,2,0:T(8,128)} fusion(bf16[16,512,1024]{2,1,0:T(8,128)(2,1)} %all-gather.5.cloned.1.call-done, f32[1,16,512,2,64]{2,4,3,1,0:T(8,128)} %fusion.71, f32[1,16,512,2,64]{2,4,3,1,0:T(8,128)} %get-tuple-element.41, f32[1,16,512,2,64]{2,4,3,1,0:T(8,128)} %get-tuple-element.40), kind=kOutput, calls=%fused_computation.111 | convolution fusion | flops 6448742400 | bytes 30932992 | tf_op jit(solution)/shard_map/bsd,ibshk->idhk/dot_general | solution.py:109
  1165.9 107.8 %reduce-scatter.11.cloned.1.call-done = f32[16,64,1024]{2,1,0:T(8,128)} async-done(((f32[16,512,1024]{2,1,0:T(8,128)}), f32[16,64,1024]{2,1,0:T(8,128)}) %reduce-scatter.11.cloned.1.call-update) | async-done | bytes 4194320 | tf_op jit(solution)/shard_map/reduce_scatter | solution.py:111
  1277.4 21.7 %all-reduce = (f32[2,1024]{1,0:T(2,128)S(1)}, f32[4,1024]{1,0:T(4,128)S(1)}) all-reduce(f32[2,1024]{1,0:T(2,128)S(1)} %pad_maximum_fusion.3, f32[4,1024]{1,0:T(4,128)S(1)} %pad_maximum_fusion.2), channel_id=1, replica_groups=mesh['dp'=2,'tp'=8] {'tp'}, use_global_device_ids=true, to_apply=%region_17.18 | all-reduce | flops 6144 | bytes 49152 | tf_op jit(solution)/shard_map/psum | solution.py:112
  (135 shorter events, 122.0 us)
Async XLA Ops:
  7.2 421.7 %copy-start = (bf16[1024,512]{1,0:T(8,128)(2,1)S(1)}, bf16[1024,512]{1,0:T(8,128)(2,1)}, u32[]{:S(2)}) copy-start(bf16[1024,512]{1,0:T(8,128)(2,1)} %param.26) | copy-start | bytes 3145732
  7.2 91.9 %all-gather.5.cloned.1.call-start = ((), (), s32[]{:S(2)}) async-start(), calls=%async_computation.4 | async-start | bytes 18874368 | tf_op jit(solution)/shard_map/all_gather | solution.py:64
  9.4 89.7 %copy-start.33 = (f32[3,2,64]{2,1,0:T(2,128)S(1)}, f32[3,2,64]{2,1,0:T(2,128)}, u32[]{:S(2)}) copy-start(f32[3,2,64]{2,1,0:T(2,128)} %param.21) | copy-start | bytes 4612
  14.5 326.2 %reduce-scatter.5.cloned.1.call-start = ((), (), s32[]{:S(2)}) async-start(), calls=%async_computation.5 | async-start | bytes 37748736 | tf_op jit(solution)/shard_map/reduce_scatter | solution.py:74
  15.0 105.6 %copy-start.10 = (f32[512,64]{0,1:T(8,128)}, f32[512,64]{0,1:T(8,128)S(1)}, u32[]{:S(2)}) copy-start(f32[512,64]{0,1:T(8,128)S(1)} %get-tuple-element.46) | copy-start | bytes 393220
  15.0 105.6 %copy-start.12 = (f32[512,64]{0,1:T(8,128)}, f32[512,64]{0,1:T(8,128)S(1)}, u32[]{:S(2)}) copy-start(f32[512,64]{0,1:T(8,128)S(1)} %get-tuple-element.44) | copy-start | bytes 393220
  174.4 166.3 %copy-start.27 = (f32[1024]{0:T(1024)S(1)}, f32[1024]{0:T(1024)}, u32[]{:S(2)}) copy-start(f32[1024]{0:T(1024)} %param.23) | copy-start | bytes 12292
  174.5 170.5 %copy-start.22 = (f32[1024]{0:T(1024)S(1)}, f32[1024]{0:T(1024)}, u32[]{:S(2)}) copy-start(f32[1024]{0:T(1024)} %param.24) | copy-start | bytes 12292
  174.5 170.4 %copy-start.29 = (f32[1024]{0:T(1024)S(1)}, f32[1024]{0:T(1024)}, u32[]{:S(2)}) copy-start(f32[1024]{0:T(1024)} %param.25) | copy-start | bytes 12292
  174.5 254.4 %all-gather.7.cloned.1.call-start = ((), (), s32[]{:S(2)}) async-start(), calls=%async_computation.6 | async-start | bytes 18874368 | tf_op jit(solution)/shard_map/all_gather | solution.py:77
  344.9 84.0 %copy-start.34 = (f32[512]{0:T(512)S(1)}, f32[512]{0:T(512)}, u32[]{:S(2)}) copy-start(f32[512]{0:T(512)} %param.27) | copy-start | bytes 6148
  347.1 164.8 %all-gather.9.cloned.1.call-start = ((), (), s32[]{:S(2)}) async-start(), calls=%async_computation.8 | async-start | bytes 18874368 | tf_op jit(solution)/shard_map/all_gather | solution.py:85
  347.8 164.2 %copy-start.31 = (bf16[512,1024]{1,0:T(8,128)(2,1)S(1)}, bf16[512,1024]{1,0:T(8,128)(2,1)}, u32[]{:S(2)}) copy-start(bf16[512,1024]{1,0:T(8,128)(2,1)} %param.28) | copy-start | bytes 3145732
  347.8 371.1 %reduce-scatter.9.cloned.1.call-start = ((), (), s32[]{:S(2)}) async-start(), calls=%async_computation.9 | async-start | bytes 37748736 | tf_op jit(solution)/shard_map/reduce_scatter | solution.py:94
  552.6 334.6 %reduce-scatter.7.cloned.1.call-start = ((), (), s32[]{:S(2)}) async-start(), calls=%async_computation.7 | async-start | bytes 37748736 | tf_op jit(solution)/shard_map/reduce_scatter | solution.py:83
  571.4 147.5 %copy-start.6 = (bf16[16,64,1024]{2,1,0:T(8,128)(2,1)S(1)}, bf16[16,64,1024]{2,1,0:T(8,128)(2,1)}, u32[]{:S(2)}) copy-start(bf16[16,64,1024]{2,1,0:T(8,128)(2,1)} %copy-done.5) | copy-start | bytes 6291460
  571.5 315.7 %copy-start.30 = (f32[1024]{0:T(1024)S(1)}, f32[1024]{0:T(1024)}, u32[]{:S(2)}) copy-start(f32[1024]{0:T(1024)} %param.29) | copy-start | bytes 12292
  571.5 407.9 %all-gather.11.cloned.1.call-start = ((), (), s32[]{:S(2)}) async-start(), calls=%async_computation.10 | async-start | bytes 18874368 | tf_op jit(solution)/shard_map/all_gather | solution.py:98
  897.6 81.8 %copy-start.15 = (bf16[2,64,1024]{2,1,0:T(8,128)(2,1)S(1)}, bf16[2,64,1024]{2,1,0:T(8,128)(2,1)}, u32[]{:S(2)}) copy-start(bf16[2,64,1024]{2,1,0:T(8,128)(2,1)} %param.22) | copy-start | bytes 786436
  897.7 376.1 %reduce-scatter.11.cloned.1.call-start = ((), (), s32[]{:S(2)}) async-start(), calls=%async_computation.11 | async-start | bytes 37748736 | tf_op jit(solution)/shard_map/reduce_scatter | solution.py:111
  1150.3 123.4 %copy-start.4 = (bf16[16,64,1024]{2,1,0:T(8,128)(2,1)S(1)}, bf16[16,64,1024]{2,1,0:T(8,128)(2,1)}, u32[]{:S(2)}) copy-start(bf16[16,64,1024]{2,1,0:T(8,128)(2,1)} %param.15) | copy-start | bytes 6291460
  1150.3 123.4 %copy-start.17 = (f32[16,64]{1,0:T(8,128)S(1)}, f32[16,64]{1,0:T(8,128)}, u32[]{:S(2)}) copy-start(f32[16,64]{1,0:T(8,128)} %copy-done.16) | copy-start | bytes 12292
  1150.3 123.4 %copy-start.19 = (f32[16,64]{1,0:T(8,128)S(1)}, f32[16,64]{1,0:T(8,128)}, u32[]{:S(2)}) copy-start(f32[16,64]{1,0:T(8,128)} %copy-done.18) | copy-start | bytes 12292
  1150.3 123.4 %copy-start.21 = (f32[1024]{0:T(1024)S(1)}, f32[1024]{0:T(1024)}, u32[]{:S(2)}) copy-start(f32[1024]{0:T(1024)} %param.18) | copy-start | bytes 12292
  (23 other events, 264.8 us)
Sparse Core Ops, SparseCore 0:
  14.7 84.3 all-gather.4
  174.6 166.0 reduce-scatter.4
  347.3 81.5 all-gather.6
  430.3 81.6 all-gather.8
  552.7 166.0 reduce-scatter.8
  721.1 166.0 reduce-scatter.6
  897.8 81.5 all-gather.10
  1107.6 166.0 reduce-scatter.10
where the time goes:
time: 1320 us; the launch traced here: 1310 us
  waiting for transfers between devices  877 us (66%)
  matrix products  301 us (23%)
  other arithmetic  87.7 us (7%)
  blocking collectives  21.7 us (2%)
  between operations  15 us (1%)
    reduce_scatter x1, waiting for transfers between devices, device_step(): lax.psum_scatter(attn_part, 'tp', scatter_dimension=1, tiled=True)  166 us
    reduce_scatter x1, waiting for transfers between devices, device_step(): mlp_sum = lax.psum_scatter(mlp_part, 'tp', scatter_dimension=1, tiled=True)  164 us
    reduce_scatter x1, waiting for transfers between devices, device_step(): d_h2 = lax.psum_scatter(d_h2_part, 'tp', scatter_dimension=1, tiled=True)  147 us
    reduce_scatter x1, waiting for transfers between devices, device_step(): d_h1 = lax.psum_scatter(d_h1_part, 'tp', scatter_dimension=1, tiled=True)  108 us
    all_gather x1, waiting for transfers between devices, device_step(): lax.all_gather(h1_f.astype(jnp.bfloat16), 'tp', axis=1, tiled=True)  83.3 us
    all_gather x1, waiting for transfers between devices, device_step(): lax.all_gather(h2_f.astype(jnp.bfloat16), 'tp', axis=1, tiled=True)  81 us
    all_gather x1, waiting for transfers between devices, device_step(): lax.all_gather(d_x1.astype(jnp.bfloat16), 'tp', axis=1, tiled=True)  63.6 us
    all_gather x1, waiting for transfers between devices, device_step(): dy_full = lax.all_gather(grad_y, 'tp', axis=1, tiled=True)  63.1 us
  transfers between devices with their start and end apart: 8, of which 8 were waited for; matrix products, arithmetic and copies ran while one was open for 9% of the time, Pallas kernels for 0%

commit v1 on v0

v1 whole, which is shorter than its diff:
```python
import jax
import jax.numpy as jnp
from jax import lax
from jax.sharding import PartitionSpec as P

LN_EPS = 1e-5
ROPE_BASE = 10000.0
INV_SQRT2 = 0.7071067811865476
INV_SQRT_2PI = 0.3989422804014327
NEG_LARGE = -1e30
F32 = jnp.float32
BF16 = jnp.bfloat16


def layer_norm(values, ln_gain, ln_bias):
    centered = values - jnp.mean(values, axis=-1, keepdims=True)
    inv_std = lax.rsqrt(jnp.mean(centered * centered, axis=-1, keepdims=True) + LN_EPS)
    x_hat = centered * inv_std
    return x_hat * ln_gain + ln_bias, x_hat, inv_std


def layer_norm_grad(d_out, x_hat, inv_std, ln_gain):
    d_hat = d_out * ln_gain
    return inv_std * (d_hat - jnp.mean(d_hat, axis=-1, keepdims=True) - x_hat * jnp.mean(d_hat * x_hat, axis=-1, keepdims=True))


def rope_tables(seq_len, head_dim):
    half_dim = head_dim // 2
    inv_freq = ROPE_BASE ** (-2.0 * jnp.arange(half_dim, dtype=F32) / head_dim)
    angles = jnp.arange(seq_len, dtype=F32)[:, None] * inv_freq[None, :]
    angles = jnp.concatenate([angles, angles], axis=-1)
    return jnp.cos(angles)[:, None, :], jnp.sin(angles)[:, None, :]


def rotate(tensor, cos_tab, sin_tab):
    half_dim = tensor.shape[-1] // 2
    swapped = jnp.concatenate([-tensor[..., half_dim:], tensor[..., :half_dim]], axis=-1)
    return tensor * cos_tab + swapped * sin_tab


def rotate_back(grad_in, cos_tab, sin_tab):
    half_dim = grad_in.shape[-1] // 2
    scaled = grad_in * sin_tab
    swapped = jnp.concatenate([scaled[..., half_dim:], -scaled[..., :half_dim]], axis=-1)
    return grad_in * cos_tab + swapped


def dot(spec, a, b):
    return jnp.einsum(spec, a, b, preferred_element_type=F32)


def solution(mesh):
    n_tp = mesh.shape['tp']
    act_spec = P('dp', 'tp', None)
    rep_vec = P(None)
    part_vec = P('dp')
    in_specs = (act_spec, act_spec, P('dp', None), rep_vec, rep_vec, P(None, None, 'tp', None), P(None, 'tp', None),
                P('tp', None, None), rep_vec, rep_vec, rep_vec, P(None, 'tp'), P('tp'), P('tp', None), rep_vec)
    out_specs = (act_spec, act_spec, part_vec, part_vec, P('dp', None, 'tp', None), P('dp', 'tp', None),
                 P(('dp', 'tp'), None, None), part_vec, part_vec, part_vec, P('dp', 'tp'), P(('dp', 'tp')),
                 P(('dp', 'tp'), None), part_vec)

    def device_step(x_in, grad_y, pad_mask, ln1_gain, ln1_bias, w_qkv, b_qkv, w_out, b_out, ln2_gain, ln2_bias, w_up, b_up, w_down, b_down):
        batch, shard_len, dim = x_in.shape
        seq_len = pad_mask.shape[1]
        _, _, heads, head_dim = w_qkv.shape
        seqs = batch // n_tp
        ffn = w_up.shape[1]
        tok = seqs * seq_len
        me = lax.axis_index('tp')
        q_scale = head_dim ** -0.5

        def to_seq(t):
            return lax.all_to_all(t, 'tp', split_axis=0, concat_axis=1, tiled=True)

        def to_pos(t):
            return lax.all_to_all(t, 'tp', split_axis=1, concat_axis=0, tiled=True)

        def gather(t):
            return lax.all_gather(t, 'tp', axis=0, tiled=False)

        x_seq = to_seq(x_in)
        w_q3 = gather(w_qkv.transpose(0, 2, 3, 1).reshape(3, heads * head_dim, dim))
        small = gather(jnp.concatenate([b_qkv.reshape(-1), b_up]))
        b_qkv_all = small[:, :3 * heads * head_dim].reshape(n_tp, 3, 1, heads * head_dim)
        b_up_all = small[:, 3 * heads * head_dim:].reshape(-1)
        w_o = gather(w_out.reshape(heads * head_dim, dim)).reshape(-1, dim)
        w_u = gather(w_up)
        dy = to_seq(grad_y).reshape(tok, dim)
        w_d = gather(w_down).reshape(-1, dim)
        mask = lax.dynamic_slice_in_dim(pad_mask, me * seqs, seqs, 0)
        key_ok = (mask > 0)[None, :, None, None, :]
        cos_tab, sin_tab = rope_tables(seq_len, head_dim)

        x_f = x_seq.reshape(tok, dim).astype(F32)
        h1_f, x_hat1, inv_std1 = layer_norm(x_f, ln1_gain, ln1_bias)
        h1 = h1_f.astype(BF16)
        qkv = dot('td,gind->igtn', h1, w_q3) + b_qkv_all.swapaxes(0, 1)
        qkv = qkv.reshape(3, n_tp, seqs, seq_len, heads, head_dim)
        q_rot = rotate(qkv[0] * q_scale, cos_tab, sin_tab).astype(BF16)
        k_rot = rotate(qkv[1], cos_tab, sin_tab).astype(BF16)
        v_heads = qkv[2].astype(BF16)
        scores = dot('gbqhk,gbshk->gbhqs', q_rot, k_rot)
        probs = jax.nn.softmax(jnp.where(key_ok, scores, NEG_LARGE), axis=-1)
        probs_low = probs.astype(BF16)
        attn_o = dot('gbhqs,gbshk->bqghk', probs_low, v_heads).astype(BF16).reshape(tok, -1)
        x1_f = (x_f + (dot('tn,nd->td', attn_o, w_o) + b_out)).astype(BF16).astype(F32)
        h2_f, x_hat2, inv_std2 = layer_norm(x1_f, ln2_gain, ln2_bias)
        h2 = h2_f.astype(BF16)
        pre_act = dot('td,gdf->tgf', h2, w_u).reshape(tok, -1) + b_up_all
        erf_term = lax.erf(pre_act * INV_SQRT2)
        act_b = (0.5 * pre_act * (1.0 + erf_term)).astype(BF16)
        gelu_slope = 0.5 * (1.0 + erf_term) + pre_act * jnp.exp(-0.5 * pre_act * pre_act) * INV_SQRT_2PI

        def scatter(t):
            return lax.psum_scatter(t, 'tp', scatter_dimension=0, tiled=True)

        grad_w_down = scatter(dot('tf,td->fd', act_b, dy))
        d_pre = dot('td,fd->tf', dy, w_d) * gelu_slope
        d_pre_b = d_pre.astype(BF16).reshape(tok, n_tp, ffn)
        grad_w_up = scatter(dot('td,tgf->gdf', h2, d_pre_b).reshape(n_tp * dim, ffn))
        mlp_sum = dot('tf,fd->td', act_b, w_d)
        y_out = to_pos((x1_f + (mlp_sum + b_down)).astype(BF16).reshape(seqs, seq_len, dim))
        d_h2 = dot('tgf,gdf->td', d_pre_b, w_u)
        dy_f = dy.astype(F32)
        d_x1 = dy_f + layer_norm_grad(d_h2, x_hat2, inv_std2, ln2_gain)
        d_x1_b = d_x1.astype(BF16)
        grad_w_out = scatter(dot('tn,td->nd', attn_o, d_x1_b))
        d_o = dot('td,nd->tn', d_x1_b, w_o).astype(BF16).reshape(seqs, seq_len, n_tp, heads, head_dim)
        d_value = dot('gbhqs,bqghk->gbshk', probs_low, d_o)
        d_probs = dot('bqghk,gbshk->gbhqs', d_o, v_heads)
        d_scores = (probs * (d_probs - jnp.sum(d_probs * probs, axis=-1, keepdims=True))).astype(BF16)
        d_query = dot('gbhqs,gbshk->gbqhk', d_scores, k_rot)
        d_key = dot('gbhqs,gbqhk->gbshk', d_scores, q_rot)
        d_qkv = jnp.stack([rotate_back(d_query, cos_tab, sin_tab) * q_scale, rotate_back(d_key, cos_tab, sin_tab), d_value])
        d_qkv_b = d_qkv.astype(BF16).reshape(3, n_tp, tok, heads * head_dim)
        grad_w_qkv = scatter(dot('igtn,td->gind', d_qkv_b, h1).reshape(n_tp * 3 * heads * head_dim, dim))
        d_h1 = dot('igtn,gind->td', d_qkv_b, w_q3)
        grad_x = to_pos((d_x1 + layer_norm_grad(d_h1, x_hat1, inv_std1, ln1_gain)).astype(BF16).reshape(seqs, seq_len, dim))
        vec = jnp.concatenate([
            jnp.sum(d_h1 * x_hat1, axis=0), jnp.sum(d_h1, axis=0), jnp.sum(d_x1, axis=0),
            jnp.sum(d_h2 * x_hat2, axis=0), jnp.sum(d_h2, axis=0), jnp.sum(dy_f, axis=0)])
        part = jnp.concatenate([
            jnp.sum(d_qkv, axis=(2, 3)).swapaxes(0, 1).reshape(n_tp, -1),
            jnp.sum(d_pre, axis=0).reshape(n_tp, -1)], axis=1)
        total = lax.psum(jnp.concatenate([vec, part.reshape(-1)]), 'tp')
        vec = total[:6 * dim].reshape(6, dim)
        part = lax.dynamic_slice_in_dim(total[6 * dim:].reshape(n_tp, -1), me, 1, 0)[0]
        grad_b_qkv = part[:3 * heads * head_dim].reshape(3, heads, head_dim)
        grad_b_up = part[3 * heads * head_dim:]
        return (y_out, grad_x, vec[0], vec[1], grad_w_qkv.reshape(3, heads, head_dim, dim).transpose(0, 3, 1, 2), grad_b_qkv,
                grad_w_out.reshape(heads, head_dim, dim), vec[2], vec[3], vec[4], grad_w_up, grad_b_up, grad_w_down, vec[5])

    return jax.shard_map(device_step, mesh=mesh, in_specs=in_specs, out_specs=out_specs, check_vma=False)
```

time: 1320 us -> 858 us (0.65)
  waiting for transfers between devices: 877 us -> 161 us
  local copies, waits for them, and re-layouts: 9.23 us -> 226 us
  blocking collectives: 21.7 us -> 101 us
  matrix products: 301 us -> 232 us
  starting transfers between devices: 0.51 us -> 28.9 us
    reduce_scatter x4, waiting for transfers between devices: 585 us -> 117 us  [scatter(): return lax.psum_scatter(t, 'tp', scatter_dimension=0, tiled=True)]
    all_gather x4, waiting for transfers between devices: 291 us -> 0.05 us  [gather(): return lax.all_gather(t, 'tp', axis=0, tiled=False)]
    dot_general x17, matrix products: 267 us -> 211 us  [dot(): return jnp.einsum(spec, a, b, preferred_element_type=F32)]
    all_gather x0 -> x1, blocking collectives: none -> 55.7 us  [gather(): return lax.all_gather(t, 'tp', axis=0, tiled=False)]
    another operation x0 -> x7, local copies, waits for them, and re-layouts: none -> 52.7 us  [device_step(): jnp.stack([rotate_back(d_query, cos_tab, sin_tab) * q_scale, rotate_back(...]
    reshape x0 -> x12, local copies, waits for them, and re-layouts: none -> 50.5 us  [the longest x1 17.6 us: device_step(): pre_act = dot('td,gdf->tgf', h2, w_u).reshape(tok, -1) + b_up_all]
    all_to_all x0 -> x4, waiting for transfers between devices: none -> 41.2 us  [the longest x2 23.7 us: to_seq(): return lax.all_to_all(t, 'tp', split_axis=0, concat_axis=1, tiled=True)]
    squeeze x1 -> x4, local copies, waits for them, and re-layouts: 2.9 us -> 42.7 us  [the longest x2 21.4 us: device_step(): k_rot = rotate(qkv[1], cos_tab, sin_tab).astype(BF16)]
  transfers between devices with their start and end apart: 8 -> 12, of which waited for: 8 -> 4; matrix products, arithmetic and copies ran while one was open for 9% -> 53% of each run, Pallas kernels for 0% -> 0%
where the time goes in v1:
time: 858 us; the launch traced here: 850 us
  matrix products  232 us (27%)
  local copies, waits for them, and re-layouts  226 us (26%)
  waiting for transfers between devices  161 us (19%)
  blocking collectives  101 us (12%)
  other arithmetic  85.6 us (10%)
  starting transfers between devices  28.9 us (3%)
  between operations  15.3 us (2%)
    dot_general x17, matrix products, dot(): return jnp.einsum(spec, a, b, preferred_element_type=F32)  211 us
    reduce_scatter x4, waiting for transfers between devices, scatter(): return lax.psum_scatter(t, 'tp', scatter_dimension=0, tiled=True)  117 us
    all_gather x1, blocking collectives, gather(): return lax.all_gather(t, 'tp', axis=0, tiled=False)  55.7 us
    another operation x7, local copies, waits for them, and re-layouts, device_step(): jnp.stack([rotate_back(d_query, cos_tab, sin_tab) * q_scale, rotate_back(...  52.7 us
    psum x1, blocking collectives, device_step(): total = lax.psum(jnp.concatenate([vec, part.reshape(-1)]), 'tp')  45.6 us
    transpose x2, local copies, waits for them, and re-layouts, dot(): return jnp.einsum(spec, a, b, preferred_element_type=F32)  28.2 us
    convert_element_type x1, other arithmetic, device_step(): (probs * (d_probs - jnp.sum(d_probs * probs, axis=-1, keepdims=True))).as...  27.4 us
    all_to_all x2, waiting for transfers between devices, to_seq(): return lax.all_to_all(t, 'tp', split_axis=0, concat_axis=1, tiled=True)  23.7 us
  transfers between devices with their start and end apart: 12, of which 4 were waited for; matrix products, arithmetic and copies ran while one was open for 53% of the time, Pallas kernels for 0%

profile of v1, /device:TPU:113, one launch (start us, length us, event | category | flops | bytes accessed | tf_op | source)
XLA Modules:
  0.0 849.6 jit_solution(4296700990932624072)
XLA Ops:
  16.4 55.7 %all-gather.3 = f32[8,1,896]{2,1,0:T(1,128)S(1)} all-gather(f32[1,1,896]{2,1,0:T(1,128)S(1)} %reshape.285), channel_id=2, replica_groups=mesh['dp'=2,'tp'=8] {'tp'}, dimensions={0}, use_global_device_ids=true | all-gather | bytes 32256 | tf_op jit(solution)/shard_map/all_gather | solution.py:80
  88.6 23.7 %all-to-all-done.2 = bf16[16,64,1024]{2,1,0:T(8,128)(2,1)} async-done(((bf16[16,64,1024]{2,1,0:T(8,128)(2,1)}), bf16[16,64,1024]{2,1,0:T(8,128)(2,1)}, u32[]{:S(2)}, u32[]{:S(2)}) %all-to-all-start.2) | async-done | bytes 2097184 | tf_op jit(solution)/shard_map/all_to_all | solution.py:74
  159.0 12.2 %copy.96 = f32[8,2,512,2,64]{2,4,3,1,0:T(8,128)} copy(f32[8,2,512,2,64]{4,3,2,1,0:T(2,128)} %reshape.297) | data formatting | bytes 8388608 | tf_op jit(solution)/shard_map/squeeze | solution.py:101
  180.3 12.2 %copy.93 = f32[8,2,512,2,64]{2,4,3,1,0:T(8,128)} copy(f32[8,2,512,2,64]{4,3,2,1,0:T(2,128)} %reshape.296) | data formatting | bytes 8388608 | tf_op jit(solution)/shard_map/squeeze | solution.py:100
  203.6 20.2 %fusion.78 = (f32[8,2,2,512]{3,2,1,0:T(2,128)S(1)}, f32[8,2,2,512,512]{3,4,2,1,0:T(8,128)}) fusion(bf16[8,2,512,2,64]{2,4,3,1,0:T(8,128)(2,1)S(1)} %get-tuple-element.45, bf16[8,2,512,2,64]{2,4,3,1,0:T(8,128)(2,1)} %get-tuple-element.44, pred[2,512]{1,0:T(4,128)(4,1)S(1)} %dynamic-slice_compare_fusion), kind=kOutput, calls=%fused_computation.139 | convolution fusion | flops 1098908160 | bytes 37815296 | tf_op jit(solution)/shard_map/sub | solution.py:104
  223.8 19.1 %fusion.70 = bf16[8,2,2,512,512]{3,4,2,1,0:T(8,128)(2,1)} fusion(f32[8,2,2,512,512]{3,4,2,1,0:T(8,128)} %get-tuple-element.58, f32[8,2,2,512]{3,2,1,0:T(2,128)S(1)} %get-tuple-element.57), kind=kLoop, calls=%fused_computation.132 | loop fusion | flops 16777216 | bytes 50397184 | tf_op jit(solution)/shard_map/convert_element_type | solution.py:105
  262.4 18.8 %multiply_convert_fusion.1 = (bf16[1024,8,512]{0,2,1:T(8,128)(2,1)}, f32[1024,8,512]{0,2,1:T(8,128)}) fusion(f32[8,512]{1,0:T(8,128)S(1)} %get-tuple-element.56, bf16[8,1024,512]{2,1,0:T(8,128)(2,1)} %bitcast.219, bf16[1024,1024]{1,0:T(8,128)(2,1)S(1)} %get-tuple-element.60, f32[1024]{0:T(1024)S(1)} %copy-done.51, f32[1024]{0:T(1024)S(1)} %copy-done.43, ...), kind=kOutput, calls=%fused_computation.15 | convolution fusion | flops 8621391872 | bytes 35684352 | tf_op jit(solution)/shard_map/td,gdf->tgf/dot_general | solution.py:49
  281.2 17.6 %copy.107 = f32[1024,4096]{1,0:T(8,128)} copy(f32[1024,4096]{0,1:T(8,128)} %bitcast.198) | data formatting | bytes 33554432 | tf_op jit(solution)/shard_map/reshape | solution.py:110
  298.9 19.3 %fusion.73 = (f32[4096]{0:T(1024)}, bf16[1024,4096]{1,0:T(8,128)(2,1)}) fusion(f32[1024,4096]{1,0:T(8,128)} %copy.107, f32[4096]{0:T(1024)S(1)} %bitcast.216, bf16[1024,1024]{1,0:T(8,128)(2,1)S(1)} %bitcast.204, bf16[4096,1024]{1,0:T(8,128)(2,1)} %all-gather.15.cloned.1.call-done), kind=kOutput, calls=%fused_computation.134 | convolution fusion | flops 8640262144 | bytes 35684352 | tf_op jit(solution)/shard_map/td,fd->tf/dot_general | solution.py:49
  318.1 12.0 %copy.153 = bf16[1024,4096]{0,1:T(8,128)(2,1)} copy(bf16[1024,4096]{1,0:T(8,128)(2,1)} %get-tuple-element.25) | data formatting | bytes 16777216 | tf_op jit(solution)/shard_map/reshape | solution.py:120
  330.1 16.7 %fusion.32 = (f32[1024]{0:T(1024)}, f32[1024]{0:T(1024)S(1)}, f32[1024]{0:T(1024)S(1)}, f32[1024]{0:T(1024)}, f32[1024,1024,1]{1,0,2:T(8,128)S(1)}) fusion(bf16[1024,1024]{1,0:T(8,128)(2,1)} %copy-done.17, f32[1024]{0:T(1024)S(1)} %add_rsqrt_fusion.1, f32[1024]{0:T(1024)S(1)} %broadcast_multiply_fusion.7, f32[1024]{0:T(1024)S(1)} %copy-done.43, ...), kind=kOutput, calls=%fused_computation.40 | convolution fusion | flops 8600416256 | bytes 23097344 | tf_op jit(solution)/shard_map/tgf,gdf->td/dot_general | solution.py:49
  370.1 23.2 %multiply_reduce_fusion = (f32[8,2,2,512]{3,2,1,0:T(2,128)S(1)}, f32[8,2,2,512,512]{3,4,2,1,0:T(8,128)}) fusion(f32[8,2,2,512,512]{3,4,2,1,0:T(8,128)} %get-tuple-element.58, f32[8,2,2,512]{3,2,1,0:T(2,128)S(1)} %get-tuple-element.57, bf16[2,512,8,2,64]{1,4,3,0,2:T(8,128)(2,1)S(1)} %copy.110, bf16[8,2,512,2,64]{2,1,4,3,0:T(2,128)(2,1)} %convert_element_type.88), kind=kOutput, calls=%fused_computation.2 | convolution fusion | flops 1098891264 | bytes 71434240 | tf_op jit(solution)/shard_map/bqghk,gbshk->gbhqs/dot_general | solution.py:49
  393.4 27.4 %multiply_convert_fusion = bf16[8,2,2,512,512]{3,4,2,1,0:T(8,128)(2,1)} fusion(f32[8,2,2,512,512]{3,4,2,1,0:T(8,128)} %get-tuple-element.66, f32[8,2,2,512]{3,2,1,0:T(2,128)S(1)} %get-tuple-element.65, f32[8,2,2,512,512]{3,4,2,1,0:T(8,128)} %get-tuple-element.58, f32[8,2,2,512]{3,2,1,0:T(2,128)S(1)} %get-tuple-element.57), kind=kLoop, calls=%fused_computation.1 | loop fusion | flops 33554432 | bytes 84017152 | tf_op jit(solution)/shard_map/convert_element_type | solution.py:132
  420.8 13.6 %bitcast_convert_fusion = (bf16[8,2,512,2,64]{2,4,3,1,0:T(8,128)(2,1)}, f32[8,2,2,64,512]{4,3,2,1,0:T(8,128)}) fusion(bf16[2,512,8,2,64]{1,4,3,0,2:T(8,128)(2,1)S(1)} %copy.110, bf16[8,2,2,512,512]{3,4,2,1,0:T(8,128)(2,1)} %fusion.70), kind=kOutput, calls=%fused_computation.57 | convolution fusion | flops 1074790400 | bytes 25165824 | tf_op jit(solution)/shard_map/gbhqs,bqghk->gbshk/dot_general | solution.py:49
  464.5 12.2 %bitcast_multiply_fusion.2 = (f32[8,2,512,2,64]{2,4,3,1,0:T(8,128)}, f32[8,2,512,2,64]{2,4,3,1,0:T(8,128)}, f32[8,2,2,64,512]{4,3,2,1,0:T(8,128)}) fusion(f32[512,64]{0,1:T(8,128)S(1)} %copy-done.22, f32[8,2,2,64,512]{4,3,2,1,0:T(8,128)} %fusion.79, bf16[8,2,512,2,64]{2,4,3,1,0:T(8,128)(2,1)S(1)} %copy-done.10, ...), kind=kOutput, calls=%fused_computation.58 | convolution fusion | flops 1075838976 | bytes 35782656 | tf_op jit(solution)/shard_map/gbhqs,gbqhk->gbshk/dot_general | solution.py:49
  550.5 15.0 %convolution_bitcast_fusion = f32[8,1024,512]{1,2,0:T(8,128)} fusion(bf16[1024,8,512]{0,2,1:T(8,128)(2,1)} %bitcast.201, bf16[1024,1024]{1,0:T(8,128)(2,1)S(1)} %copy-done.19, f32[1024]{0:T(1024)S(1)} %copy-done.52, f32[1024]{0:T(1024)S(1)} %copy-done.44, f32[1024]{0:T(1024)S(1)} %copy-done.40, f32[1024]{0:T(1024)S(1)} %copy-done.35), kind=kOutput, calls=%fused_computation.21 | convolution fusion | flops 8596226048 | bytes 27279360 | tf_op jit(solution)/shard_map/td,tgf->gdf/dot_general | solution.py:49
  565.5 16.5 %copy.128 = f32[8,1024,512]{2,1,0:T(8,128)} copy(f32[8,1024,512]{1,2,0:T(8,128)} %convolution_bitcast_fusion) | data formatting | bytes 33554432 | tf_op jit(solution)/shard_map/td,tgf->gdf/transpose | solution.py:49
  583.6 14.7 %fusion.80 = f32[4096,1024]{1,0:T(8,128)} fusion(bf16[1024,4096]{0,1:T(8,128)(2,1)} %bitcast.225, bf16[1024,1024]{1,0:T(8,128)(2,1)S(1)} %bitcast.205), kind=kOutput, calls=%fused_computation.142 | convolution fusion | flops 8589934592 | bytes 27262976 | tf_op jit(solution)/shard_map/tf,td->fd/dot_general | solution.py:49
  599.9 13.7 %fusion.34 = bf16[1024,1024]{1,0:T(8,128)(2,1)S(1)} fusion(bf16[1024,1024]{1,0:T(8,128)(2,1)S(1)} %copy-done.20, bf16[1024,8,512]{0,2,1:T(8,128)(2,1)} %get-tuple-element.61, bf16[8,512,1024]{2,1,0:T(8,128)(2,1)} %bitcast.218, f32[1024]{0:T(1024)S(1)} %copy-done.53), kind=kOutput, calls=%fused_computation.42 | convolution fusion | flops 8594128896 | bytes 20975616 | tf_op jit(solution)/shard_map/tf,fd->td/dot_general | solution.py:49
  624.0 12.4 %fusion.40 = (f32[1024]{0:T(1024)S(1)}, f32[1024]{0:T(1024)S(1)}, f32[1024]{0:T(1024)S(1)}, f32[1024]{0:T(1024)S(1)}, f32[1024,1024,1,1]{1,0,3,2:T(8,128)S(1)}) fusion(f32[8,2,64,1024]{3,2,0,1:T(8,128)} %copy.89, f32[1024]{0:T(1024)S(1)} %copy-done.33, f32[1024]{0:T(1024)S(1)} %copy-done.31, f32[1024]{0:T(1024)S(1)} %copy-done.37, ...), kind=kOutput, calls=%fused_computation.56 | convolution fusion | flops 6451884032 | bytes 21000192 | tf_op jit(solution)/shard_map/igtn,gind->td/dot_general | solution.py:49
  641.8 17.4 %all-to-all-done.1 = bf16[2,512,1024]{2,0,1:T(2,128)(2,1)S(1)} async-done(((bf16[2,512,1024]{2,0,1:T(2,128)(2,1)}), bf16[2,512,1024]{2,0,1:T(2,128)(2,1)S(1)}, u32[]{:S(2)}, u32[]{:S(2)}) %all-to-all-start.1) | async-done | bytes 2097184 | tf_op jit(solution)/shard_map/all_to_all | solution.py:77
  672.6 45.6 %psum.7 = f32[13312]{0:T(1024)S(1)} all-reduce(f32[13312]{0:T(1024)S(1)} %constant_dynamic-update-slice_fusion.4), channel_id=1, replica_groups=mesh['dp'=2,'tp'=8] {'tp'}, use_global_device_ids=true, to_apply=%region_19.20 | all-reduce | flops 13312 | bytes 106496 | tf_op jit(solution)/shard_map/psum | solution.py:146
  725.7 26.3 %reduce-scatter.9.cloned.1.call-done = f32[1024,512]{1,0:T(8,128)} async-done(((f32[8192,512]{1,0:T(8,128)}), f32[1024,512]{1,0:T(8,128)}) %reduce-scatter.9.cloned.1.call-update) | async-done | bytes 2097168 | tf_op jit(solution)/shard_map/reduce_scatter | solution.py:116
  752.0 90.3 %reduce-scatter.11.cloned.1.call-done = f32[512,1024]{1,0:T(8,128)} async-done(((f32[4096,1024]{1,0:T(8,128)}), f32[512,1024]{1,0:T(8,128)}) %reduce-scatter.11.cloned.1.call-update) | async-done | bytes 2097168 | tf_op jit(solution)/shard_map/reduce_scatter | solution.py:116
  (224 shorter events, 278.3 us)
Async XLA Ops:
  7.2 113.7 %all-gather.9.cloned.1.call-start = ((), (), s32[]{:S(2)}) async-start(), calls=%async_computation.8 | async-start | bytes 7077888 | tf_op jit(solution)/shard_map/all_gather | solution.py:80
  8.0 247.4 %all-gather.11.cloned.1.call-start = ((), (), s32[]{:S(2)}) async-start(), calls=%async_computation.9 | async-start | bytes 2359296 | tf_op jit(solution)/shard_map/all_gather | solution.py:80
  8.8 253.5 %all-gather.13.cloned.1.call-start = ((), (), s32[]{:S(2)}) async-start(), calls=%async_computation.14 | async-start | bytes 9437184 | tf_op jit(solution)/shard_map/all_gather | solution.py:80
  9.6 62.4 %all-to-all-start = ((bf16[16,64,1024]{2,1,0:T(8,128)(2,1)}), bf16[16,64,1024]{2,1,0:T(8,128)(2,1)S(1)}, u32[]{:S(2)}, u32[]{:S(2)}) async-start(bf16[16,64,1024]{2,1,0:T(8,128)(2,1)} %param.15), calls=%async_computation | async-start | bytes 4194304 | tf_op jit(solution)/shard_map/all_to_all | solution.py:74
  15.6 283.2 %all-gather.15.cloned.1.call-start = ((), (), s32[]{:S(2)}) async-start(), calls=%async_computation.15 | async-start | bytes 9437184 | tf_op jit(solution)/shard_map/all_gather | solution.py:80
  72.1 40.2 %all-to-all-start.2 = ((bf16[16,64,1024]{2,1,0:T(8,128)(2,1)}), bf16[16,64,1024]{2,1,0:T(8,128)(2,1)}, u32[]{:S(2)}, u32[]{:S(2)}) async-start(bf16[16,64,1024]{2,1,0:T(8,128)(2,1)} %param.16), calls=%async_computation.2 | async-start | bytes 4194304 | tf_op jit(solution)/shard_map/all_to_all | solution.py:74
  81.9 643.8 %reduce-scatter.7.cloned.1.call-start = ((), (), s32[]{:S(2)}) async-start(), calls=%async_computation.11 | async-start | bytes 4718592 | tf_op jit(solution)/shard_map/reduce_scatter | solution.py:116
  83.0 116.0 %copy-start.21 = (f32[512,64]{0,1:T(8,128)}, f32[512,64]{0,1:T(8,128)S(1)}, u32[]{:S(2)}) copy-start(f32[512,64]{0,1:T(8,128)S(1)} %get-tuple-element.48) | copy-start | bytes 393220
  83.0 116.0 %copy-start.27 = (f32[512,64]{0,1:T(8,128)}, f32[512,64]{0,1:T(8,128)S(1)}, u32[]{:S(2)}) copy-start(f32[512,64]{0,1:T(8,128)S(1)} %get-tuple-element.46) | copy-start | bytes 393220
  85.8 32.1 %copy-start.30 = (f32[1024]{0:T(1024)}, f32[1024]{0:T(1024)S(1)}, u32[]{:S(2)}) copy-start(f32[1024]{0:T(1024)S(1)} %div.43) | copy-start | bytes 12292
  117.9 12.5 %copy-start.32 = (f32[1024]{0:T(1024)}, f32[1024]{0:T(1024)S(1)}, u32[]{:S(2)}) copy-start(f32[1024]{0:T(1024)S(1)} %rsqrt.20) | copy-start | bytes 12292
  203.6 20.2 %copy-start.9 = (bf16[8,2,512,2,64]{2,4,3,1,0:T(8,128)(2,1)}, bf16[8,2,512,2,64]{2,4,3,1,0:T(8,128)(2,1)S(1)}, u32[]{:S(2)}) copy-start(bf16[8,2,512,2,64]{2,4,3,1,0:T(8,128)(2,1)S(1)} %get-tuple-element.45) | copy-start | bytes 6291460
  223.8 19.2 %copy-start.25 = (bf16[8,2,512,2,64]{2,1,4,3,0:T(2,128)(2,1)S(1)}, bf16[8,2,512,2,64]{2,1,4,3,0:T(2,128)(2,1)}, u32[]{:S(2)}) copy-start(bf16[8,2,512,2,64]{2,1,4,3,0:T(2,128)(2,1)} %convert_element_type.88) | copy-start | bytes 6291460
  261.6 19.6 %copy-start.17 = (bf16[1024,1024]{1,0:T(8,128)(2,1)}, bf16[1024,1024]{1,0:T(8,128)(2,1)S(1)}, u32[]{:S(2)}) copy-start(bf16[1024,1024]{1,0:T(8,128)(2,1)S(1)} %get-tuple-element.60) | copy-start | bytes 6291460
  261.6 85.2 %copy-start.34 = (f32[1024]{0:T(1024)}, f32[1024]{0:T(1024)S(1)}, u32[]{:S(2)}) copy-start(f32[1024]{0:T(1024)S(1)} %broadcast_multiply_fusion.7) | copy-start | bytes 12292
  262.3 84.5 %copy-start.39 = (f32[1024]{0:T(1024)}, f32[1024]{0:T(1024)S(1)}, u32[]{:S(2)}) copy-start(f32[1024]{0:T(1024)S(1)} %add_rsqrt_fusion.1) | copy-start | bytes 12292
  281.2 17.6 %copy-start.15 = (bf16[8,2,64,1024]{3,2,0,1:T(8,128)(2,1)S(1)}, bf16[8,2,64,1024]{3,2,0,1:T(8,128)(2,1)}, u32[]{:S(2)}) copy-start(bf16[8,2,64,1024]{3,2,0,1:T(8,128)(2,1)} %copy.106) | copy-start | bytes 6291460
  330.1 16.7 %copy-start.18 = (bf16[1024,1024]{1,0:T(8,128)(2,1)S(1)}, bf16[1024,1024]{1,0:T(8,128)(2,1)}, u32[]{:S(2)}) copy-start(bf16[1024,1024]{1,0:T(8,128)(2,1)} %copy-done.17) | copy-start | bytes 6291460
  370.0 355.7 %reduce-scatter.5.cloned.1.call-start = ((), (), s32[]{:S(2)}) async-start(), calls=%async_computation.10 | async-start | bytes 14155776 | tf_op jit(solution)/shard_map/reduce_scatter | solution.py:116
  549.0 203.0 %reduce-scatter.9.cloned.1.call-start = ((), (), s32[]{:S(2)}) async-start(), calls=%async_computation.12 | async-start | bytes 18874368 | tf_op jit(solution)/shard_map/reduce_scatter | solution.py:116
  582.1 260.2 %reduce-scatter.11.cloned.1.call-start = ((), (), s32[]{:S(2)}) async-start(), calls=%async_computation.13 | async-start | bytes 18874368 | tf_op jit(solution)/shard_map/reduce_scatter | solution.py:116
  617.2 42.1 %all-to-all-start.1 = ((bf16[2,512,1024]{2,0,1:T(2,128)(2,1)}), bf16[2,512,1024]{2,0,1:T(2,128)(2,1)S(1)}, u32[]{:S(2)}, u32[]{:S(2)}) async-start(bf16[2,512,1024]{2,0,1:T(2,128)(2,1)} %copy.104), calls=%async_computation.1 | async-start | bytes 4194304 | tf_op jit(solution)/shard_map/all_to_all | solution.py:77
  641.8 25.2 %copy-start.41 = (f32[4096]{0:T(1024)S(1)}, f32[4096]{0:T(1024)}, u32[]{:S(2)}) copy-start(f32[4096]{0:T(1024)} %get-tuple-element.24) | copy-start | bytes 49156
  659.3 62.9 %all-to-all-start.3 = ((bf16[2,512,1024]{2,0,1:T(2,128)(2,1)}), bf16[2,512,1024]{2,0,1:T(2,128)(2,1)}, u32[]{:S(2)}, u32[]{:S(2)}) async-start(bf16[2,512,1024]{2,0,1:T(2,128)(2,1)} %copy.122), calls=%async_computation.3 | async-start | bytes 4194304 | tf_op jit(solution)/shard_map/all_to_all | solution.py:77
  (42 other events, 211.0 us)
Sparse Core Ops, SparseCore 0:
  9.6 59.3 all-gather.8
  70.6 26.0 all-gather.10
  98.3 48.5 all-gather.12
  148.4 46.1 all-gather.14
  370.2 33.5 reduce-scatter.6
  549.1 70.5 reduce-scatter.4
  622.6 129.3 reduce-scatter.8
  754.9 87.3 reduce-scatter.10

commit v2 on v0

v2 whole, which is shorter than its diff:
```python
import functools

import jax
import jax.numpy as jnp
from jax import lax
from jax.experimental import pallas as pl
from jax.experimental.pallas import tpu as pltpu
from jax.sharding import PartitionSpec as P


LN_EPS = 1e-5
ROPE_BASE = 10000.0
INV_SQRT2 = 0.7071067811865476
INV_SQRT_2PI = 0.3989422804014327
NEG_LARGE = -1e30
F32 = jnp.float32
BF16 = jnp.bfloat16
MESH = pl.DeviceIdType.MESH
VMEM_LIMIT = 56 * 1024 * 1024
NN = (((1,), (0,)), ((), ()))
NT = (((1,), (1,)), ((), ()))
TN = (((0,), (0,)), ((), ()))


def mm(a, b, dims):
    return lax.dot_general(a, b, dims, preferred_element_type=F32)


def ln_stats(v):
    centered = v - jnp.mean(v, axis=-1, keepdims=True)
    inv_std = lax.rsqrt(jnp.mean(centered * centered, axis=-1, keepdims=True) + LN_EPS)
    return centered * inv_std, inv_std


def ln_grad(d_out, x_hat, inv_std, gain):
    d_hat = d_out * gain
    return inv_std * (d_hat - jnp.mean(d_hat, axis=-1, keepdims=True) - x_hat * jnp.mean(d_hat * x_hat, axis=-1, keepdims=True))


def low_half(shape, head_dim):
    lane = lax.broadcasted_iota(jnp.int32, shape, 1)
    return (lane % head_dim) < (head_dim // 2)


def swap_halves(t, head_dim):
    half = head_dim // 2
    width = t.shape[-1]
    return jnp.where(low_half(t.shape, head_dim), pltpu.roll(t, width - half, 1), pltpu.roll(t, half, 1))


def call(body, out_shape, grid, in_specs, out_specs, flops, nbytes, scratch=(), trans=0):
    return pl.pallas_call(
        body, out_shape=out_shape, grid=grid, in_specs=in_specs, out_specs=out_specs, scratch_shapes=scratch,
        compiler_params=pltpu.CompilerParams(dimension_semantics=('arbitrary',) * len(grid), vmem_limit_bytes=VMEM_LIMIT),
        cost_estimate=pl.CostEstimate(flops=flops, bytes_accessed=nbytes, transcendentals=trans))


def rep(shape):
    return pl.BlockSpec(shape, lambda *_: (0,) * len(shape))


def entry(x_in, small, n_tp):
    def body(x_src, b_src, x_out, b_out, x_send, x_recv, b_send, b_recv, own):
        me = lax.axis_index('tp')
        barrier = pltpu.get_barrier_semaphore()
        for j in range(1, n_tp):
            pl.semaphore_signal(barrier, inc=1, device_id={'tp': lax.rem(me + j, n_tp)}, device_id_type=MESH)
        pl.semaphore_wait(barrier, n_tp - 1)
        copies = []
        for j in range(1, n_tp):
            peer = lax.rem(me + j, n_tp)
            copies.append(pltpu.make_async_remote_copy(
                src_ref=b_src, dst_ref=b_out.at[me], send_sem=b_send.at[j], recv_sem=b_recv.at[j],
                device_id={'tp': peer}, device_id_type=MESH))
        for j in range(1, n_tp):
            peer = lax.rem(me + j, n_tp)
            copies.append(pltpu.make_async_remote_copy(
                src_ref=x_src.at[peer], dst_ref=x_out.at[me], send_sem=x_send.at[j], recv_sem=x_recv.at[j],
                device_id={'tp': peer}, device_id_type=MESH))
        for c in copies:
            c.start()
        mine = pltpu.make_async_copy(x_src.at[me], x_out.at[me], own)
        mine.start()
        b_out[me] = b_src[...]
        mine.wait()
        for c in copies:
            c.wait()

    sem = pltpu.SemaphoreType.DMA((n_tp,))
    return pl.pallas_call(
        body, out_shape=(jax.ShapeDtypeStruct(x_in.shape, x_in.dtype), jax.ShapeDtypeStruct((n_tp,) + small.shape, small.dtype)),
        in_specs=[pl.BlockSpec(memory_space=pl.ANY), pl.BlockSpec(memory_space=pltpu.VMEM)],
        out_specs=(pl.BlockSpec(memory_space=pl.ANY), pl.BlockSpec(memory_space=pltpu.VMEM)),
        scratch_shapes=[sem, sem, sem, sem, pltpu.SemaphoreType.DMA], name='entry',
        compiler_params=pltpu.CompilerParams(collective_id=0, has_side_effects=True, vmem_limit_bytes=VMEM_LIMIT),
        cost_estimate=pl.CostEstimate(flops=20_000_000_000, bytes_accessed=1 << 22, transcendentals=0))(x_in, small)


def qkv_body(hd, chunk, x_ref, w_ref, b_ref, cos_ref, sin_ref, gain_ref, bias_ref, h1_ref, q_ref, k_ref, v_ref):
    tok = x_ref.shape[0]
    width = q_ref.shape[2]

    @pl.when(pl.program_id(0) == 0)
    def _():
        @pl.loop(0, tok // 128)
        def _(i):
            rows = pl.ds(pl.multiple_of(i * 128, 128), 128)
            x_hat, _ = ln_stats(x_ref[rows, :].astype(F32))
            h1_ref[rows, :] = (x_hat * gain_ref[...] + bias_ref[...]).astype(BF16)

    @pl.loop(0, tok // chunk)
    def _(i):
        rows = pl.ds(pl.multiple_of(i * chunk, chunk), chunk)
        t = mm(h1_ref[rows, :], w_ref[0], NT) + b_ref[0]
        cos, sin = cos_ref[rows, :], sin_ref[rows, :]
        tq = t[:, :width] * (hd ** -0.5)
        tk = t[:, width:2 * width]
        q_ref[0, rows, :] = (tq * cos + swap_halves(tq, hd) * sin).astype(BF16)
        k_ref[0, rows, :] = (tk * cos + swap_halves(tk, hd) * sin).astype(BF16)
        v_ref[0, rows, :] = t[:, 2 * width:].astype(BF16)


def attn_fwd_body(hd, qc, len_ref, q_ref, k_ref, v_ref, o_ref, m_ref, l_ref):
    n_src, _, p_len, width = q_ref.shape[1:]
    seq = n_src * p_len
    heads = width // hd
    key_ok = lax.broadcasted_iota(jnp.int32, (seq, 1), 0) < len_ref[pl.program_id(1)]
    k = k_ref[...].reshape(seq, width)
    v_t = v_ref[...].reshape(seq, width).T
    lane = lax.broadcasted_iota(jnp.int32, (qc, width), 1)
    srcs = qc // p_len
    for c in range(seq // qc):
        q = q_ref[0, c * srcs:(c + 1) * srcs, 0].reshape(qc, width)
        outs = []
        for h in range(heads):
            q_h = jnp.where(lane // hd == h, q, jnp.zeros_like(q))
            s = jnp.where(key_ok, mm(k, q_h, NT), NEG_LARGE)
            m = jnp.max(s, axis=0, keepdims=True)
            e = jnp.exp(s - m)
            r = 1.0 / jnp.sum(e, axis=0, keepdims=True)
            p = (e * r).astype(BF16)
            outs.append(mm(v_t[h * hd:(h + 1) * hd], p, NN))
            m_ref[0, 0, h:h + 1, c * qc:(c + 1) * qc] = m
            l_ref[0, 0, h:h + 1, c * qc:(c + 1) * qc] = r
        o = jnp.concatenate(outs, axis=0).T.astype(BF16)
        o_ref[c * srcs:(c + 1) * srcs, 0] = o.reshape(srcs, p_len, width)


def attn_bwd_body(hd, qc, len_ref, q_ref, k_ref, v_ref, do_ref, m_ref, l_ref, cos_ref, sin_ref, d_ref, bsum_ref, dk_acc, dv_acc, dq_acc):
    n_src, _, p_len, width = q_ref.shape[1:]
    seq = n_src * p_len
    heads = width // hd
    key_ok = lax.broadcasted_iota(jnp.int32, (seq, 1), 0) < len_ref[pl.program_id(1)]
    k = k_ref[...].reshape(seq, width)
    v = v_ref[...].reshape(seq, width)
    k_t = k.T
    lane = lax.broadcasted_iota(jnp.int32, (qc, width), 1)
    srcs = qc // p_len
    for c in range(seq // qc):
        q = q_ref[0, c * srcs:(c + 1) * srcs, 0].reshape(qc, width)
        d_o = do_ref[c * srcs:(c + 1) * srcs, 0].reshape(qc, width)
        dk = jnp.zeros((seq, width), F32)
        dv = jnp.zeros((seq, width), F32)
        dqs = []
        for h in range(heads):
            mine = lane // hd == h
            q_h = jnp.where(mine, q, jnp.zeros_like(q))
            do_h = jnp.where(mine, d_o, jnp.zeros_like(d_o))
            cols = slice(c * qc, (c + 1) * qc)
            s = jnp.where(key_ok, mm(k, q_h, NT), NEG_LARGE)
            p = jnp.exp(s - m_ref[0, 0, h:h + 1, cols]) * l_ref[0, 0, h:h + 1, cols]
            dv += mm(p.astype(BF16), do_h, NN)
            dp = mm(v, do_h, NT)
            ds = (p * (dp - jnp.sum(dp * p, axis=0, keepdims=True))).astype(BF16)
            dk += mm(ds, q_h, NN)
            dqs.append(mm(k_t[h * hd:(h + 1) * hd], ds, NN))
        dq_acc[c * qc:(c + 1) * qc, :] = jnp.concatenate(dqs, axis=0).T
        if c == 0:
            dk_acc[...] = dk
            dv_acc[...] = dv
        else:
            dk_acc[...] += dk
            dv_acc[...] += dv
    cos, sin = cos_ref[...], sin_ref[...]
    dq, dk, dv = dq_acc[...], dk_acc[...], dv_acc[...]
    dtq = (dq * cos - swap_halves(dq, hd) * sin) * (hd ** -0.5)
    dtk = dk * cos - swap_halves(dk, hd) * sin
    for i, t in enumerate((dtq, dtk, dv)):
        d_ref[0, :, 0, :, i * width:(i + 1) * width] = t.astype(BF16).reshape(n_src, p_len, width)
        bsum_ref[0, 0, i:i + 1, :] = jnp.sum(t, axis=0, keepdims=True)


def proj_body(x_ref, o_ref, w_ref, bo_ref, gain_ref, bias_ref, x1_ref, h2_ref):
    w = w_ref[...].reshape(-1, w_ref.shape[2])
    x1 = (x_ref[...].astype(F32) + (mm(o_ref[...], w, NN) + bo_ref[...])).astype(BF16)
    x1_ref[...] = x1
    x_hat, _ = ln_stats(x1.astype(F32))
    h2_ref[...] = (x_hat * gain_ref[...] + bias_ref[...]).astype(BF16)


def up_body(chunk, h2_ref, w_ref, b_ref, dy_ref, act_ref, slope_ref, gw_ref):
    @pl.loop(0, h2_ref.shape[0] // chunk)
    def _(i):
        rows = pl.ds(pl.multiple_of(i * chunk, chunk), chunk)
        pre = mm(h2_ref[rows, :], w_ref[0], NN) + b_ref[0]
        erf_term = lax.erf(pre * INV_SQRT2)
        act_ref[rows, :] = (0.5 * pre * (1.0 + erf_term)).astype(BF16)
        slope_ref[rows, :] = 0.5 * (1.0 + erf_term) + pre * jnp.exp(-0.5 * pre * pre) * INV_SQRT_2PI

    gw_ref[0] = mm(act_ref[...], dy_ref[...], TN)


def dpre_body(chunk, dy_ref, w_ref, slope_ref, h2_ref, dpre_ref, gw_ref, gb_ref):
    gb_ref[...] = jnp.zeros_like(gb_ref)

    @pl.loop(0, dy_ref.shape[0] // chunk)
    def _(i):
        rows = pl.ds(pl.multiple_of(i * chunk, chunk), chunk)
        d_pre = mm(dy_ref[rows, :], w_ref[0], NT) * slope_ref[rows, :]
        gb_ref[0] += jnp.sum(d_pre, axis=0, keepdims=True)
        dpre_ref[rows, :] = d_pre.astype(BF16)

    gw_ref[0] = mm(h2_ref[...], dpre_ref[...], TN)


def down_body(chunk, act_ref, wd_ref, dpre_ref, wu_ref, x1_ref, dy_ref, wo_ref, bd_ref, gain_ref,
              y_ref, dx1_ref, dx1b_ref, do_ref, sums_ref, y_acc, dh_acc):
    g = pl.program_id(0)
    y_new = mm(act_ref[...], wd_ref[0], NN)
    dh_new = mm(dpre_ref[...], wu_ref[0], NT)

    @pl.when(g == 0)
    def _():
        y_acc[...] = y_new
        dh_acc[...] = dh_new

    @pl.when(g > 0)
    def _():
        y_acc[...] += y_new
        dh_acc[...] += dh_new

    @pl.when(g == pl.num_programs(0) - 1)
    def _():
        sums_ref[...] = jnp.zeros_like(sums_ref)

        @pl.loop(0, y_acc.shape[0] // chunk)
        def _(i):
            rows = pl.ds(pl.multiple_of(i * chunk, chunk), chunk)
            x1 = x1_ref[rows, :].astype(F32)
            dy = dy_ref[rows, :].astype(F32)
            dh = dh_acc[rows, :]
            y_ref[rows, :] = (x1 + (y_acc[rows, :] + bd_ref[...])).astype(BF16)
            x_hat, inv_std = ln_stats(x1)
            d_x1 = dy + ln_grad(dh, x_hat, inv_std, gain_ref[...])
            dx1_ref[rows, :] = d_x1
            low = d_x1.astype(BF16)
            dx1b_ref[rows, :] = low
            do_ref[rows, :] = mm(low, wo_ref[...].reshape(-1, wo_ref.shape[2]), NT).astype(BF16)
            for n, t in enumerate((d_x1, dh * x_hat, dh, dy)):
                sums_ref[n:n + 1, :] += jnp.sum(t, axis=0, keepdims=True)


def final_body(n_tp, chunk, d_ref, w_ref, h1_ref, o_ref, dx1b_ref, dx1_ref, x_ref, gain_ref, sums_ref, bsum_ref, gb_ref,
               gx_ref, gw_ref, dh_acc, vec):
    s = pl.program_id(0)
    n3 = d_ref.shape[2]
    width = o_ref.shape[1]
    n_b = bsum_ref.shape[2]

    @pl.when(s == 0)
    def _():
        dh_acc[...] = mm(d_ref[0], w_ref[0], NN)

    @pl.when(jnp.logical_and(s > 0, s < n_tp))
    def _():
        dh_acc[...] += mm(d_ref[0], w_ref[0], NN)

    @pl.when(s == n_tp - 1)
    def _():
        vec[...] = jnp.zeros_like(vec)
        vec[2:6, :] = sums_ref[0:4, :]

        @pl.loop(0, dh_acc.shape[0] // chunk)
        def _(i):
            rows = pl.ds(pl.multiple_of(i * chunk, chunk), chunk)
            x_hat, inv_std = ln_stats(x_ref[rows, :].astype(F32))
            dh = dh_acc[rows, :]
            gx_ref[rows, :] = (dx1_ref[rows, :] + ln_grad(dh, x_hat, inv_std, gain_ref[...])).astype(BF16)
            vec[0:1, :] += jnp.sum(dh * x_hat, axis=0, keepdims=True)
            vec[1:2, :] += jnp.sum(dh, axis=0, keepdims=True)

    @pl.when(s >= n_tp)
    def _():
        gw_ref[0, 0:n3, :] = mm(d_ref[0], h1_ref[...], TN)
        gw_ref[0, n3:n3 + width, :] = mm(o_ref[...], dx1b_ref[...], TN)
        gw_ref[0, n3 + width:, :] = vec[...]
        gw_ref[0, n3 + width + 6:n3 + width + 7, 0:n_b] = bsum_ref[0]
        gw_ref[0, n3 + width + 6:n3 + width + 7, n_b:n_b + gb_ref.shape[2]] = gb_ref[0]


def rope_tables(seq_len, head_dim):
    half_dim = head_dim // 2
    inv_freq = ROPE_BASE ** (-2.0 * jnp.arange(half_dim, dtype=F32) / head_dim)
    angles = jnp.arange(seq_len, dtype=F32)[:, None] * inv_freq[None, :]
    cos, sin = jnp.cos(angles), jnp.sin(angles)
    return jnp.concatenate([cos, cos], axis=-1), jnp.concatenate([-sin, sin], axis=-1)


def solution(mesh):
    n_tp = mesh.shape['tp']
    act_spec = P('dp', 'tp', None)
    rep_vec = P(None)
    part_vec = P('dp')
    in_specs = (act_spec, act_spec, P('dp', None), rep_vec, rep_vec, P(None, None, 'tp', None), P(None, 'tp', None),
                P('tp', None, None), rep_vec, rep_vec, rep_vec, P(None, 'tp'), P('tp'), P('tp', None), rep_vec)
    out_specs = (act_spec, act_spec, part_vec, part_vec, P('dp', None, 'tp', None), P('dp', 'tp', None),
                 P(('dp', 'tp'), None, None), part_vec, part_vec, part_vec, P('dp', 'tp'), P(('dp', 'tp')),
                 P(('dp', 'tp'), None), part_vec)

    def device_step(x_in, grad_y, pad_mask, ln1_gain, ln1_bias, w_qkv, b_qkv, w_out, b_out, ln2_gain, ln2_bias, w_up, b_up, w_down, b_down):
        batch, p_len, dim = x_in.shape
        seq_len = pad_mask.shape[1]
        _, _, heads, hd = w_qkv.shape
        seqs = batch // n_tp
        ffn = w_up.shape[1]
        width = heads * hd
        n3 = 3 * width
        tok = seqs * seq_len
        me = lax.axis_index('tp')
        sds = jax.ShapeDtypeStruct

        def exchange(t):
            return lax.all_to_all(t, 'tp', split_axis=0, concat_axis=0, tiled=True)

        w_att = jnp.concatenate([w_qkv.transpose(0, 2, 3, 1).reshape(n3, dim), w_out.reshape(width, dim)], axis=0)
        w_att = lax.all_gather(w_att, 'tp', axis=0, tiled=False)
        pad = -(n3 + ffn) % 1024
        small = jnp.concatenate([b_qkv.reshape(-1), b_up, jnp.zeros((pad,), F32)]).reshape(-1, 128)
        x, small = entry(x_in.reshape(n_tp, seqs * p_len, dim), small, n_tp)
        x = x.reshape(tok, dim)
        small = small.reshape(n_tp, 1, -1)
        b_att, b_ffn = small[:, :, :n3], small[:, :, n3:n3 + ffn]
        w_u = lax.all_gather(w_up, 'tp', axis=0, tiled=False)
        x, grad_y = lax.optimization_barrier((x, grad_y))
        dy = exchange(grad_y).reshape(tok, dim)
        w_d = lax.all_gather(w_down, 'tp', axis=0, tiled=False)
        lens = jnp.sum((lax.dynamic_slice_in_dim(pad_mask, me * seqs, seqs, 0) > 0).astype(jnp.int32), axis=1)
        cos, sin = rope_tables(seq_len, hd)
        cos, sin = jnp.tile(cos, (1, heads)), jnp.tile(sin, (1, heads))

        def by_token(t):
            return jnp.broadcast_to(t.reshape(n_tp, 1, p_len, width), (n_tp, seqs, p_len, width)).reshape(tok, width)

        row = lambda t: t.reshape(1, dim)
        full = rep((tok, dim))
        vec = rep((1, dim))
        per_head = pl.BlockSpec((1, tok, width), lambda g: (g, 0, 0))
        w_spec = pl.BlockSpec((1, n3, dim), lambda g: (g, 0, 0))
        h1, q, k, v = call(
            functools.partial(qkv_body, hd, 256),
            (sds((tok, dim), BF16),) + (sds((n_tp, tok, width), BF16),) * 3, (n_tp,),
            [full, w_spec, pl.BlockSpec((1, 1, n3), lambda g: (g, 0, 0)), rep((tok, width)), rep((tok, width)), vec, vec],
            (full, per_head, per_head, per_head), 2 * tok * dim * n3 * n_tp, 2 * (tok * dim * 5 + n_tp * n3 * dim),
        )(x, w_att, b_att, by_token(cos), by_token(sin), row(ln1_gain), row(ln1_bias))

        five = (n_tp, n_tp, seqs, p_len, width)
        q5, k5, v5 = (t.reshape(five) for t in (q, k, v))
        head_blk = pl.BlockSpec((1, n_tp, 1, p_len, width), lambda g, b, *_: (g, 0, b, 0, 0))
        o_blk = pl.BlockSpec((n_tp, 1, p_len, width), lambda g, b, *_: (0, b, 0, g))
        stat_blk = pl.BlockSpec((1, 1, heads, seq_len), lambda g, b, *_: (g, b, 0, 0))
        stat = sds((n_tp, seqs, heads, seq_len), F32)
        att_flops = n_tp * seqs * heads * seq_len * seq_len * hd * 2
        o, m_stat, l_stat = pl.pallas_call(
            functools.partial(attn_fwd_body, hd, 256), name='attn_fwd',
            out_shape=(sds((n_tp, seqs, p_len, n_tp * width), BF16), stat, stat),
            grid_spec=pltpu.PrefetchScalarGridSpec(
                num_scalar_prefetch=1, grid=(n_tp, seqs), in_specs=[head_blk] * 3, out_specs=(o_blk, stat_blk, stat_blk)),
            compiler_params=pltpu.CompilerParams(dimension_semantics=('arbitrary', 'arbitrary'), vmem_limit_bytes=VMEM_LIMIT),
            cost_estimate=pl.CostEstimate(flops=8 * att_flops, bytes_accessed=8 * tok * dim, transcendentals=att_flops // 128),
        )(lens, q5, k5, v5)
        o = o.reshape(tok, n_tp * width)

        rows = pl.BlockSpec((256, dim), lambda i: (i, 0))
        wo_spec = pl.BlockSpec((n_tp, width, dim), lambda *_: (0, n3 // width, 0))
        x1, h2 = call(proj_body, (sds((tok, dim), BF16),) * 2, (tok // 256,), [rows, rows, wo_spec, vec, vec, vec], (rows, rows),
                      2 * tok * dim * dim, 8 * tok * dim)(x, o, w_att, row(b_out), row(ln2_gain), row(ln2_bias))

        cols = pl.BlockSpec((tok, ffn), lambda g: (0, g))
        wu_spec = pl.BlockSpec((1, dim, ffn), lambda g: (g, 0, 0))
        wd_spec = pl.BlockSpec((1, ffn, dim), lambda g: (g, 0, 0))
        b_spec = pl.BlockSpec((1, 1, ffn), lambda g: (g, 0, 0))
        mlp_flops = 2 * tok * dim * ffn * n_tp
        act, slope, gw_down = call(
            functools.partial(up_body, 512), (sds((tok, n_tp * ffn), BF16), sds((tok, n_tp * ffn), F32), sds((n_tp, ffn, dim), F32)), (n_tp,),
            [full, wu_spec, b_spec, full], (cols, cols, wd_spec), 2 * mlp_flops, 60 << 20)(h2, w_u, b_ffn, dy)
        scatter = lambda t: lax.psum_scatter(t.reshape(-1, t.shape[-1]), 'tp', scatter_dimension=0, tiled=True)
        grad_w_down = scatter(gw_down)
        d_pre, gw_up, gb_up = call(
            functools.partial(dpre_body, 512), (sds((tok, n_tp * ffn), BF16), sds((n_tp, dim, ffn), F32), sds((n_tp, 1, ffn), F32)), (n_tp,),
            [full, wd_spec, cols, full], (cols, wu_spec, b_spec), 2 * mlp_flops, 60 << 20)(dy, w_d, slope, h2)
        grad_w_up = scatter(gw_up)
        y, d_x1, d_x1b, d_o, sums = call(
            functools.partial(down_body, 256),
            (sds((tok, dim), BF16), sds((tok, dim), F32), sds((tok, dim), BF16), sds((tok, n_tp * width), BF16), sds((8, dim), F32)), (n_tp,),
            [cols, wd_spec, cols, wu_spec, full, full, wo_spec, vec, vec],
            (full, full, full, full, rep((8, dim))), 2 * mlp_flops, 60 << 20,
            scratch=[pltpu.VMEM((tok, dim), F32), pltpu.VMEM((tok, dim), F32)],
        )(act, w_d, d_pre, w_u, x1, dy, w_att, row(b_down), row(ln2_gain))
        y_out = exchange(y.reshape(batch, p_len, dim))

        d_qkv, bsum = pl.pallas_call(
            functools.partial(attn_bwd_body, hd, 256), name='attn_bwd',
            out_shape=(sds((n_tp, n_tp, seqs, p_len, n3), BF16), sds((n_tp, seqs, 3, width), F32)),
            grid_spec=pltpu.PrefetchScalarGridSpec(
                num_scalar_prefetch=1, grid=(n_tp, seqs),
                in_specs=[head_blk] * 3 + [o_blk, stat_blk, stat_blk, rep((seq_len, width)), rep((seq_len, width))],
                out_specs=(pl.BlockSpec((1, n_tp, 1, p_len, n3), lambda g, b, *_: (g, 0, b, 0, 0)),
                           pl.BlockSpec((1, 1, 3, width), lambda g, b, *_: (g, b, 0, 0))),
                scratch_shapes=[pltpu.VMEM((seq_len, width), F32)] * 3),
            compiler_params=pltpu.CompilerParams(dimension_semantics=('arbitrary', 'arbitrary'), vmem_limit_bytes=VMEM_LIMIT),
            cost_estimate=pl.CostEstimate(flops=20 * att_flops, bytes_accessed=16 * tok * dim, transcendentals=att_flops // 128),
        )(lens, q5, k5, v5, d_o.reshape(n_tp, seqs, p_len, n_tp * width), m_stat, l_stat, cos, sin)

        y_out, d_qkv = lax.optimization_barrier((y_out, d_qkv))
        first = lambda s: (jnp.minimum(s, n_tp - 1), 0, 0)
        second = lambda s: jnp.maximum(s - n_tp, 0)
        n_rows = n3 + width + 8
        grad_x, gw_att = call(
            functools.partial(final_body, n_tp, 256), (sds((tok, dim), BF16), sds((n_tp, n_rows, dim), F32)), (2 * n_tp,),
            [pl.BlockSpec((1, tok, n3), lambda s: (lax.rem(s, n_tp), 0, 0)), pl.BlockSpec((1, n3, dim), first), full,
             pl.BlockSpec((tok, width), lambda s: (0, second(s))), full, full, full, vec, rep((8, dim)),
             pl.BlockSpec((1, 1, n3), lambda s: (second(s), 0, 0)), pl.BlockSpec((1, 1, ffn), lambda s: (second(s), 0, 0))],
            (full, pl.BlockSpec((1, n_rows, dim), lambda s: (second(s), 0, 0))), 2 * tok * dim * (2 * n3 + width) * n_tp, 40 << 20,
            scratch=[pltpu.VMEM((tok, dim), F32), pltpu.VMEM((8, dim), F32)],
        )(d_qkv.reshape(n_tp, tok, n3), w_att, h1, o, d_x1b, d_x1, x, row(ln1_gain), sums,
          jnp.sum(bsum, axis=1).reshape(n_tp, 1, n3), gb_up)
        grad_x = exchange(grad_x.reshape(batch, p_len, dim))
        tail = scatter(gw_att)
        grad_w_qkv = tail[:n3].reshape(3, heads, hd, dim).transpose(0, 3, 1, 2)
        grad_w_out = tail[n3:n3 + width].reshape(heads, hd, dim)
        vecs = tail[n3 + width:]
        grad_b_qkv = vecs[6, :n3].reshape(3, heads, hd)
        grad_b_up = vecs[6, n3:n3 + ffn]
        return (y_out, grad_x, vecs[0], vecs[1], grad_w_qkv, grad_b_qkv, grad_w_out, vecs[2], vecs[3], vecs[4], grad_w_up,
                grad_b_up, grad_w_down, vecs[5])

    return jax.shard_map(device_step, mesh=mesh, in_specs=in_specs, out_specs=out_specs, check_vma=False)
```

time: 1320 us -> 648 us (0.49)
  waiting for transfers between devices: 877 us -> 292 us
  matrix products: 301 us -> 0 us
  Pallas kernels: 0 us -> 297 us
  other arithmetic: 87.7 us -> 5.34 us
  blocking collectives: 21.7 us -> 0 us
  starting transfers between devices: 0.51 us -> 16.3 us
    reduce_scatter x4 -> x3, waiting for transfers between devices: 585 us -> 240 us  [device_step(): lax.psum_scatter(t.reshape(-1, t.shape[-1]), 'tp', scatter_dimension=0, t...]
    pallas_call x0 -> x9, Pallas kernels: none -> 297 us  [the longest x1 49.7 us: entry(): pl.pallas_call(body, out_shape=(jax.ShapeDtypeStruct(x_in.shape, x_in.dty...]
    all_gather x4 -> x3, waiting for transfers between devices: 291 us -> 12.1 us  [the longest x1 12.1 us: device_step(): w_att = lax.all_gather(w_att, 'tp', axis=0, tiled=False)]
    dot_general x17 -> x0, matrix products: 267 us -> none  [the longest x1 23.3 us: device_step(): jnp.einsum('bqhk,bshk->bhqs', d_attn_o, v_heads, preferred_element_type=j...]
    convert_element_type x6 -> x0, other arithmetic: 44.1 us -> none  [the longest x1 27.6 us: device_step(): (attn_probs * (d_probs - jnp.sum(d_probs * attn_probs, axis=-1, keepdims=...]
    all_to_all x0 -> x3, waiting for transfers between devices: none -> 37.8 us  [exchange(): return lax.all_to_all(t, 'tp', split_axis=0, concat_axis=0, tiled=True)]
    sub x2 -> x0, matrix products: 34.1 us -> none  [device_step(): attn_probs = jax.nn.softmax(jnp.where(key_ok, scores, NEG_LARGE), axis=-1)]
    reduce_sum x8 -> x2, other arithmetic: 28.4 us -> 2.14 us  [the longest x1 1.36 us: device_step(): jnp.sum((lax.dynamic_slice_in_dim(pad_mask, me * seqs, seqs, 0) > 0).asty...]
  transfers between devices with their start and end apart: 8 -> 9, of which waited for: 8 -> 5; matrix products, arithmetic and copies ran while one was open for 9% -> 3% of each run, Pallas kernels for 0% -> 30%
where the time goes in v2:
time: 648 us; the launch traced here: 646 us
  Pallas kernels  297 us (46%)
  waiting for transfers between devices  292 us (45%)
  local copies, waits for them, and re-layouts  20.7 us (3%)
  starting transfers between devices  16.3 us (3%)
  between operations  14.2 us (2%)
    reduce_scatter x3, waiting for transfers between devices, device_step(): lax.psum_scatter(t.reshape(-1, t.shape[-1]), 'tp', scatter_dimension=0, t...  240 us
    pallas_call x1, Pallas kernels, entry(): pl.pallas_call(body, out_shape=(jax.ShapeDtypeStruct(x_in.shape, x_in.dty...  49.7 us
    pallas_call x1, Pallas kernels, device_step(): pl.pallas_call(functools.partial(attn_bwd_body, hd, 256), name='attn_bwd'...  44.9 us
    pallas_call x1, Pallas kernels, device_step(): call(functools.partial(down_body, 256), (sds((tok, dim), BF16), sds((tok,...  39 us
    pallas_call x1, Pallas kernels, device_step(): pl.pallas_call(functools.partial(attn_fwd_body, hd, 256), name='attn_fwd'...  37.8 us
    all_to_all x3, waiting for transfers between devices, exchange(): return lax.all_to_all(t, 'tp', split_axis=0, concat_axis=0, tiled=True)  37.8 us
    pallas_call x1, Pallas kernels, device_step(): call(functools.partial(final_body, n_tp, 256), (sds((tok, dim), BF16), sd...  33.6 us
    pallas_call x1, Pallas kernels, device_step(): call(functools.partial(up_body, 512), (sds((tok, n_tp * ffn), BF16), sds(...  31.5 us
  transfers between devices with their start and end apart: 9, of which 5 were waited for; matrix products, arithmetic and copies ran while one was open for 3% of the time, Pallas kernels for 30%

profile of v2, /device:TPU:113, one launch (start us, length us, event | category | flops | bytes accessed | tf_op | source)
XLA Modules:
  0.0 646.1 jit_solution(4785645182849336988)
XLA Ops:
  7.3 2.3 pad_maximum_fusion
  11.9 49.7 %entry.1 = (bf16[8,128,1024]{2,1,0:T(8,128)(2,1)}, f32[8,8,128]{2,1,0:T(8,128)}) custom-call(bf16[8,128,1024]{2,1,0:T(8,128)(2,1)} %bitcast.91, f32[8,128]{1,0:T(8,128)} %maximum_bitcast_fusion.b_src), custom_call_target="tpu_custom_call" | custom-call | flops 20000000000 | bytes 4194304 | tf_op jit(solution)/shard_map/entry/pallas_call | solution.py:90
  61.6 5.5 all-to-all-start
  71.1 1.4 fusion.3.len_ref
  72.4 12.1 %all-gather.7.cloned.1.call-done = bf16[4096,1024]{1,0:T(8,128)(2,1)} async-done(((bf16[512,1024]{1,0:T(8,128)(2,1)}), bf16[4096,1024]{1,0:T(8,128)(2,1)}) %all-gather.7.cloned.1.call-update) | async-done | bytes 8388624 | tf_op jit(solution)/shard_map/all_gather | solution.py:336
  86.2 25.3 %shard_map.254 = (bf16[1024,1024]{1,0:T(8,128)(2,1)}, bf16[8,1024,128]{2,1,0:T(8,128)(2,1)}, bf16[8,1024,128]{2,1,0:T(8,128)(2,1)}, bf16[8,1024,128]{2,1,0:T(8,128)(2,1)}) custom-call(bf16[1024,1024]{1,0:T(8,128)(2,1)} %bitcast.58, bf16[8,512,1024]{2,1,0:T(8,128)(2,1)} %bitcast.52, f32[8,1,384]{2,1,0:T(1,128)} %slice.57.b_ref, f32[1024,128]{1,0:T(8,128)} %bitcast.71, ...), custom_call_target="tpu_custom_call" | custom-call | flops 6442450944 | bytes 16777216 | tf_op jit(solution)/shard_map/pallas_call | solution.py:359
  111.5 37.8 %attn_fwd.1 = (bf16[8,2,64,1024]{3,2,1,0:T(8,128)(2,1)}, f32[8,2,2,512]{3,2,1,0:T(2,128)}, f32[8,2,2,512]{3,2,1,0:T(2,128)}) custom-call(s32[2]{0:T(128)} %fusion.3.len_ref, bf16[8,8,2,64,128]{4,3,2,1,0:T(8,128)(2,1)} %bitcast.97, bf16[8,8,2,64,128]{4,3,2,1,0:T(8,128)(2,1)} %bitcast.99, bf16[8,8,2,64,128]{4,3,2,1,0:T(8,128)(2,1)} %bitcast.101), custom_call_target="tpu_custom_call" | custom-call | flops 8589934592 | bytes 8388608 | tf_op jit(solution)/shard_map/attn_fwd/pallas_call | solution.py:373
  149.3 7.5 %shard_map.255 = (bf16[1024,1024]{1,0:T(8,128)(2,1)}, bf16[1024,1024]{1,0:T(8,128)(2,1)}) custom-call(bf16[1024,1024]{1,0:T(8,128)(2,1)} %bitcast.59, bf16[1024,1024]{1,0:T(8,128)(2,1)} %bitcast.61, bf16[8,512,1024]{2,1,0:T(8,128)(2,1)} %bitcast.53, f32[1,1024]{1,0:T(1,128)} %bitcast.76, f32[1,1024]{1,0:T(1,128)} %bitcast.78, f32[1,1024]{1,0:T(1,128)} %bitcast.77), custom_call_target="tpu_custom_call" | custom-call | flops 2147483648 | bytes 8388608 | tf_op jit(solution)/shard_map/pallas_call | solution.py:385
  158.1 31.5 %shard_map.256 = (bf16[1024,4096]{1,0:T(8,128)(2,1)}, f32[1024,4096]{1,0:T(8,128)}, f32[8,512,1024]{2,1,0:T(8,128)}) custom-call(bf16[1024,1024]{1,0:T(8,128)(2,1)} %get-tuple-element.51.h2_ref, bf16[8,1024,512]{2,1,0:T(8,128)(2,1)} %bitcast.87, f32[8,1,512]{2,1,0:T(1,128)} %slice.58.b_ref, bf16[1024,1024]{1,0:T(8,128)(2,1)} %bitcast.63), custom_call_target="tpu_custom_call" | custom-call | flops 17179869184 | bytes 62914560 | tf_op jit(solution)/shard_map/pallas_call | solution.py:393
  189.6 28.0 %shard_map.257 = (bf16[1024,4096]{1,0:T(8,128)(2,1)}, f32[8,1024,512]{2,1,0:T(8,128)}, f32[8,1,512]{2,1,0:T(1,128)}) custom-call(bf16[1024,1024]{1,0:T(8,128)(2,1)} %bitcast.64, bf16[8,512,1024]{2,1,0:T(8,128)(2,1)} %bitcast.89, f32[1024,4096]{1,0:T(8,128)} %get-tuple-element.54.slope_ref, bf16[1024,1024]{1,0:T(8,128)(2,1)} %get-tuple-element.51.h2_ref), custom_call_target="tpu_custom_call" | custom-call | flops 17179869184 | bytes 62914560 | tf_op jit(solution)/shard_map/pallas_call | solution.py:398
  217.6 39.0 %shard_map.258 = (bf16[1024,1024]{1,0:T(8,128)(2,1)}, f32[1024,1024]{1,0:T(8,128)}, bf16[1024,1024]{1,0:T(8,128)(2,1)}, bf16[1024,1024]{1,0:T(8,128)(2,1)}, f32[8,1024]{1,0:T(8,128)}) custom-call(bf16[1024,4096]{1,0:T(8,128)(2,1)} %get-tuple-element.53.act_ref, bf16[8,512,1024]{2,1,0:T(8,128)(2,1)} %bitcast.90, ...), custom_call_target="tpu_custom_call" | custom-call | flops 17179869184 | bytes 62914560 | tf_op jit(solution)/shard_map/pallas_call | solution.py:402
  256.6 5.5 all-to-all-start.1
  262.2 44.9 %attn_bwd.1 = (bf16[8,8,2,64,384]{4,3,2,1,0:T(8,128)(2,1)}, f32[8,2,3,128]{3,2,1,0:T(4,128)}) custom-call(s32[2]{0:T(128)} %fusion.3.len_ref, bf16[8,8,2,64,128]{4,3,2,1,0:T(8,128)(2,1)} %bitcast.98, bf16[8,8,2,64,128]{4,3,2,1,0:T(8,128)(2,1)} %bitcast.100, bf16[8,8,2,64,128]{4,3,2,1,0:T(8,128)(2,1)} %bitcast.102, bf16[8,2,64,1024]{3,2,1,0:T(8,128)(2,1)} %bitcast.103, ...), custom_call_target="tpu_custom_call" | custom-call | flops 21474836480 | bytes 16777216 | tf_op jit(solution)/shard_map/attn_bwd/pallas_call | solution.py:411
  308.5 33.6 %shard_map.259 = (bf16[1024,1024]{1,0:T(8,128)(2,1)}, f32[8,520,1024]{2,1,0:T(8,128)}) custom-call(bf16[8,1024,384]{2,1,0:T(8,128)(2,1)} %bitcast.96, bf16[8,512,1024]{2,1,0:T(8,128)(2,1)} %bitcast.55, bf16[1024,1024]{1,0:T(8,128)(2,1)} %get-tuple-element.64.h1_ref, bf16[1024,1024]{1,0:T(8,128)(2,1)} %bitcast.62, ...), custom_call_target="tpu_custom_call" | custom-call | flops 15032385536 | bytes 41943040 | tf_op jit(solution)/shard_map/pallas_call | solution.py:428
  343.4 5.0 all-to-all-start.2
  348.3 37.8 %all-to-all-done.2 = bf16[16,64,1024]{2,1,0:T(8,128)(2,1)} async-done(((bf16[16,64,1024]{2,1,0:T(8,128)(2,1)}), bf16[16,64,1024]{2,1,0:T(8,128)(2,1)}, u32[]{:S(2)}, u32[]{:S(2)}) %all-to-all-start.2) | async-done | bytes 2097184 | tf_op jit(solution)/shard_map/all_to_all | solution.py:333
  386.1 68.5 %reduce-scatter.4.cloned.1.call-done = f32[520,1024]{1,0:T(8,128)} async-done(((f32[4160,1024]{1,0:T(8,128)}), f32[520,1024]{1,0:T(8,128)}) %reduce-scatter.4.cloned.1.call-update) | async-done | bytes 2129936 | tf_op jit(solution)/shard_map/reduce_scatter | solution.py:396
  457.3 1.9 slice.63
  459.1 2.7 slice.61
  461.9 1.7 fusion.4
  463.6 81.1 %reduce-scatter.8.cloned.1.call-done = f32[512,1024]{1,0:T(8,128)} async-done(((f32[4096,1024]{1,0:T(8,128)}), f32[512,1024]{1,0:T(8,128)}) %reduce-scatter.8.cloned.1.call-update) | async-done | bytes 2097168 | tf_op jit(solution)/shard_map/reduce_scatter | solution.py:396
  544.7 90.1 %reduce-scatter.6.cloned.1.call-done = f32[1024,512]{1,0:T(8,128)} async-done(((f32[8192,512]{1,0:T(8,128)}), f32[1024,512]{1,0:T(8,128)}) %reduce-scatter.6.cloned.1.call-update) | async-done | bytes 2097168 | tf_op jit(solution)/shard_map/reduce_scatter | solution.py:396
  634.7 1.3 copy.41
  636.1 3.1 copy.42
  (47 shorter events, 14.7 us)
Async XLA Ops:
  7.2 77.3 %all-gather.7.cloned.1.call-start = ((), (), s32[]{:S(2)}) async-start(), calls=%async_computation.9 | async-start | bytes 9437184 | tf_op jit(solution)/shard_map/all_gather | solution.py:336
  9.5 1.7 copy-start.2
  9.5 1.8 copy-start.3
  9.6 147.3 %all-gather.9.cloned.1.call-start = ((), (), s32[]{:S(2)}) async-start(), calls=%async_computation.10 | async-start | bytes 9437184 | tf_op jit(solution)/shard_map/all_gather | solution.py:343
  10.4 179.2 %all-gather.11.cloned.1.call-start = ((), (), s32[]{:S(2)}) async-start(), calls=%async_computation.11 | async-start | bytes 9437184 | tf_op jit(solution)/shard_map/all_gather | solution.py:346
  61.6 5.9 copy-start.1
  61.6 95.3 %all-to-all-start = ((bf16[16,64,1024]{2,1,0:T(8,128)(2,1)}), bf16[16,64,1024]{2,1,0:T(8,128)(2,1)S(1)}, u32[]{:S(2)}, u32[]{:S(2)}) async-start(bf16[16,64,1024]{2,1,0:T(8,128)(2,1)} %param.16), calls=%async_computation | async-start | bytes 4194304 | tf_op jit(solution)/shard_map/all_to_all | solution.py:333
  156.8 1.3 copy-start
  256.6 51.8 %all-to-all-start.1 = ((bf16[16,64,1024]{2,1,0:T(8,128)(2,1)}), bf16[16,64,1024]{2,1,0:T(8,128)(2,1)S(1)}, u32[]{:S(2)}, u32[]{:S(2)}) async-start(bf16[16,64,1024]{2,1,0:T(8,128)(2,1)} %bitcast.67), calls=%async_computation.1 | async-start | bytes 4194304 | tf_op jit(solution)/shard_map/all_to_all | solution.py:333
  262.2 192.4 %reduce-scatter.4.cloned.1.call-start = ((), (), s32[]{:S(2)}) async-start(), calls=%async_computation.6 | async-start | bytes 19169280 | tf_op jit(solution)/shard_map/reduce_scatter | solution.py:396
  342.1 202.6 %reduce-scatter.8.cloned.1.call-start = ((), (), s32[]{:S(2)}) async-start(), calls=%async_computation.8 | async-start | bytes 18874368 | tf_op jit(solution)/shard_map/reduce_scatter | solution.py:396
  342.7 292.0 %reduce-scatter.6.cloned.1.call-start = ((), (), s32[]{:S(2)}) async-start(), calls=%async_computation.7 | async-start | bytes 18874368 | tf_op jit(solution)/shard_map/reduce_scatter | solution.py:396
  343.4 42.7 %all-to-all-start.2 = ((bf16[16,64,1024]{2,1,0:T(8,128)(2,1)}), bf16[16,64,1024]{2,1,0:T(8,128)(2,1)}, u32[]{:S(2)}, u32[]{:S(2)}) async-start(bf16[16,64,1024]{2,1,0:T(8,128)(2,1)} %bitcast.66), calls=%async_computation.2 | async-start | bytes 4194304 | tf_op jit(solution)/shard_map/all_to_all | solution.py:333
Sparse Core Ops, SparseCore 0:
  10.2 74.2 all-gather.6
  86.1 47.9 all-gather.8
  135.7 46.4 all-gather.10
  342.2 112.3 reduce-scatter.3
  457.3 87.2 reduce-scatter.7
  547.4 87.2 reduce-scatter.5

commit v3 on v0

v3 whole, which is shorter than its diff:
```python
import functools

import jax
import jax.numpy as jnp
from jax import lax
from jax.experimental import pallas as pl
from jax.experimental.pallas import tpu as pltpu
from jax.sharding import PartitionSpec as P

LN_EPS = 1e-5
ROPE_BASE = 10000.0
INV_SQRT2 = 0.7071067811865476
INV_SQRT_2PI = 0.3989422804014327
NEG_LARGE = -1e30
F32 = jnp.float32
BF16 = jnp.bfloat16
VMEM_LIMIT = 66_500_000
LANES = 128
NN = (((1,), (0,)), ((), ()))
NT = (((1,), (1,)), ((), ()))
TN = (((0,), (0,)), ((), ()))
ANY = pl.BlockSpec(memory_space=pl.ANY)


def mm(a, b, dims):
    return lax.dot_general(a, b, dims, preferred_element_type=F32)


def ln_stats(v):
    centered = v - jnp.mean(v, axis=-1, keepdims=True)
    inv_std = lax.rsqrt(jnp.mean(centered * centered, axis=-1, keepdims=True) + LN_EPS)
    return centered * inv_std, inv_std


def ln_grad(d_out, x_hat, inv_std, gain):
    d_hat = d_out * gain
    return inv_std * (d_hat - jnp.mean(d_hat, axis=-1, keepdims=True) - x_hat * jnp.mean(d_hat * x_hat, axis=-1, keepdims=True))


def col_sum(t):
    return jnp.sum(t, axis=0, keepdims=True)


def swap_halves(t, head_dim):
    half = head_dim // 2
    lane = lax.broadcasted_iota(jnp.int32, t.shape, t.ndim - 1)
    return jnp.where(lane % head_dim < half, pltpu.roll(t, t.shape[-1] - half, t.ndim - 1), pltpu.roll(t, half, t.ndim - 1))


def span(i, n):
    return pl.ds(pl.multiple_of(i * n, n), n)


def loop_rows(total, n, body):
    @pl.loop(0, total // n)
    def _(i):
        body(span(i, n))


class Net:
    def __init__(self, n_tp, send, recv, local):
        self.n_tp, self.send, self.recv, self.local = n_tp, send, recv, local
        self.copies, self.count, self.n_local = {}, 0, 0

    def peer(self, chip, core):
        me = lax.axis_index('tp')
        at = lax.rem(me + 2 * chip, self.n_tp) if chip else me
        return at + 1 - 2 * lax.rem(at, 2) if core else at

    def add(self, name, src, dst, chip, core=0):
        n = self.count
        self.count += 1

        def make():
            return pltpu.make_async_remote_copy(
                src_ref=src(), dst_ref=dst(), send_sem=self.send.at[n], recv_sem=self.recv.at[n],
                device_id={'tp': self.peer(chip, core)}, device_id_type=pl.DeviceIdType.MESH)

        self.copies.setdefault(name, []).append(make)

    def add_local(self, name, src, dst):
        n = self.n_local
        self.n_local += 1
        self.copies.setdefault(name, []).append(lambda: pltpu.make_async_copy(src(), dst(), self.local.at[n]))

    def start(self, *names):
        for name in names:
            for make in self.copies[name]:
                make().start()

    def got(self, *names):
        for name in names:
            for make in self.copies[name]:
                make().wait_recv()

    def sent(self, *names):
        for name in names:
            for make in self.copies[name]:
                make().wait_send()

    def done(self, *names):
        for name in names:
            for make in self.copies[name]:
                make().wait()

    def gather(self, name, own, buf):
        rows = own.shape[0]
        top, bot, whole = pl.ds(0, rows // 2), pl.ds(rows // 2, rows // 2), pl.ds(0, rows)

        def put(stage, src, slot, part, chip, core=0):
            take = (lambda: own.at[part]) if src is None else (lambda: buf.at[src, part])
            self.add(name + stage, take, lambda: buf.at[slot, part], chip, core)

        put('_a', None, 6, top, 1)
        put('_a', None, 2, bot, 3)
        put('_b', None, 6, bot, 1)
        put('_b', None, 2, top, 3)
        put('_b', None, 1, whole, 0, 1)
        put('_relay', 6, 4, top, 1)
        put('_relay', 2, 4, bot, 3)
        put('_fwd', 6, 7, whole, 0, 1)
        put('_fwd', 2, 3, whole, 0, 1)
        put('_last', 4, 5, whole, 0, 1)

    def exchange(self, name, src, dst, rows):
        me = lax.axis_index('tp')
        for core in range(2):
            for chip in (1, 3, 2, 0):
                if chip + core:
                    self.add(name, lambda c=chip, k=core: src.at[span(self.peer(c, k), rows)], lambda: dst.at[span(me, rows)], chip, core)
        self.add_local(name + '_own', lambda: src.at[span(me, rows)], lambda: dst.at[span(me, rows)])

    def scatter(self, name, p, got, summed, out):
        half = p.shape[1] // 2
        top, bot = pl.ds(0, half), pl.ds(half, half)
        self.add(name + '_relay', lambda: p.at[2, top], lambda: got.at[0], 1)
        self.add(name + '_relay', lambda: p.at[2, bot], lambda: got.at[1], 3)
        self.add(name + '_next', lambda: p.at[1, bot], lambda: out.at[0, bot], 1)
        self.add(name + '_prev', lambda: p.at[3, top], lambda: out.at[1, top], 3)
        self.add(name + '_sum', lambda: summed.at[0], lambda: out.at[0, top], 1)
        self.add(name + '_sum', lambda: summed.at[1], lambda: out.at[1, bot], 3)


def solution(mesh):
    n_tp = mesh.shape['tp']
    n_chips = n_tp // 2
    act_spec = P('dp', 'tp', None)
    rep_vec = P(None)
    part_vec = P('dp')
    in_specs = (act_spec, act_spec, P('dp', None), rep_vec, rep_vec, P(None, None, 'tp', None), P(None, 'tp', None),
                P('tp', None, None), rep_vec, rep_vec, rep_vec, P(None, 'tp'), P('tp'), P('tp', None), rep_vec)
    out_specs = (act_spec, act_spec, part_vec, part_vec, P('dp', None, 'tp', None), P('dp', 'tp', None),
                 P(('dp', 'tp'), None, None), part_vec, part_vec, part_vec, P('dp', 'tp'), P(('dp', 'tp')),
                 P(('dp', 'tp'), None), part_vec)

    def device_step(x_in, grad_y, pad_mask, ln1_gain, ln1_bias, w_qkv, b_qkv, w_out, b_out, ln2_gain, ln2_bias, w_up, b_up, w_down, b_down):
        batch, p_len, dim = x_in.shape
        seq = pad_mask.shape[1]
        _, _, heads, hd = w_qkv.shape
        seqs = batch // n_tp
        ffn = w_up.shape[1]
        width = heads * hd
        n3 = 3 * width
        tok = seqs * seq
        chunk = seqs * p_len
        qc = seq // 2
        q_scale = hd ** -0.5
        sds = jax.ShapeDtypeStruct
        n_tile = n3 + width
        n_rows = n_tile + 16
        half = dim // 2

        def kernel(x_ref, dy_ref, mask_ref, wq_ref, bq_ref, wo_ref, wu_ref, bu_ref, wd_ref, vecs_ref, freq_ref,
                   y_out, gx_out, g_att, g_up, g_down, g_vec,
                   wq, wu, wd, q_hbm, k_hbm, v_hbm, act_hbm, slope_hbm, p_dn, p_up, p_at, got_dn, got_up, got_at,
                   sum_dn, sum_up, sum_at, r_dn, r_up, r_at,
                   x, h1, dy, o4, x1, h2, wo, dx1b, do4, acc, acc2, p_rcv, p_snd, t_got, t_own, d4, dq_acc, dk_acc, dv_acc,
                   cos_t, sin_t, ok, m_st, l_st, b_att, b_ffn, b_all, u_all, gb, vec, vec_all, dpre,
                   send, recv, local, pair_send, pair_recv, pair_ready):
            net = Net(n_tp, send, recv, local)
            me = lax.axis_index('tp')
            gain1, bias1, bias_o, gain2, bias2, bias_d = (vecs_ref[i:i + 1, :] for i in range(6))

            net.gather('wq', wq_ref, wq)
            net.gather('wo', wo_ref, wo)
            net.gather('wu', wu_ref, wu)
            net.gather('wd', wd_ref, wd)
            net.exchange('x', x_ref, x, chunk)
            net.exchange('dy', dy_ref, dy, chunk)
            net.exchange('y', x1, y_out, chunk)
            net.exchange('gx', h1, gx_out, chunk)
            for chip in range(n_chips):
                for core in range(2):
                    if chip + core:
                        slot = 2 * (-chip % n_chips) + core
                        net.add('bias', lambda: bq_ref, lambda n=slot: b_all.at[n], chip, core)
                        net.add('bias', lambda: bu_ref, lambda n=slot: u_all.at[n], chip, core)
                        net.add('vec', lambda: vec, lambda n=slot: vec_all.at[n], chip, core)
            net.scatter('dn', p_dn, got_dn, sum_dn, r_dn)
            net.scatter('up', p_up, got_up, sum_up, r_up)
            net.scatter('at', p_at, got_at, sum_at, r_at)
            for name, ref, tmp, buf in (('wq', wq_ref, lambda: h2.at[pl.ds(0, n3)], wq), ('wu', wu_ref, lambda: x1.at[:, pl.ds(0, ffn)], wu),
                                        ('wd', wd_ref, lambda: dx1b.at[pl.ds(0, ffn)], wd)):
                net.add_local('load', lambda r=ref: r, tmp)
                net.add_local('store', tmp, lambda b=buf: b.at[0])
            net.add_local('own', lambda: wo_ref, lambda: wo.at[0])
            net.add_local('own', lambda: bq_ref, lambda: b_all.at[0])
            net.add_local('own', lambda: bu_ref, lambda: u_all.at[0])
            parts = {'dn': (p_dn, got_dn, sum_dn, n_tile), 'up': (p_up, got_up, sum_up, n_tile), 'at': (p_at, got_at, sum_at, n_rows)}
            for name, (p, got, summed, rows) in parts.items():
                h = rows // 2
                for i, (j, lo) in enumerate(((1, 0), (3, h))):
                    net.add_local(name + '_load', lambda g=got, i=i: g.at[i], lambda i=i, h=h: t_got.at[i, pl.ds(0, h)])
                    net.add_local(name + '_load', lambda p=p, j=j, lo=lo, h=h: p.at[j, pl.ds(lo, h)], lambda i=i, h=h: t_own.at[i, pl.ds(0, h)])
                    net.add_local(name + '_store', lambda i=i, h=h: t_own.at[i, pl.ds(0, h)], lambda s=summed, i=i: s.at[i])

            def add_relayed(name):
                h = parts[name][3] // 2
                net.done(name + '_load')

                def body(rows):
                    for i in range(2):
                        t_own[i, rows] += t_got[i, rows]

                loop_rows(h, 8, body)
                net.start(name + '_store')

            def hooks(step, table):
                for at, act in table.items():
                    @pl.when(step == at)
                    def _(act=act):
                        act()

            tile_order = (2, 1, 3, 0)

            def place(i):
                return jnp.where(i == 0, 2, jnp.where(i == 1, 1, jnp.where(i == 2, 3, 0)))

            def order(s):
                return 2 * place(lax.rem(s, n_chips)) + 1 - lax.div(s, n_chips)

            def pair(s, name, tile, rows):
                n = n_chips
                base = n * list(parts).index(name)
                p = parts[name][0]

                def copy(i):
                    return pltpu.make_async_remote_copy(
                        src_ref=p_snd.at[lax.rem(i, 2), pl.ds(0, rows)], dst_ref=p_rcv.at[i, pl.ds(0, rows)],
                        send_sem=pair_send.at[base + i], recv_sem=pair_recv.at[base + i],
                        device_id={'tp': net.peer(0, 1)}, device_id_type=pl.DeviceIdType.MESH)

                @pl.when(jnp.logical_and(s >= 1, s <= n))
                def _():
                    copy(s - 1).start()

                @pl.when(jnp.logical_and(s >= 2, s < n))
                def _():
                    copy(s - 2).wait_send()

                @pl.when(s < n)
                def _():
                    tile(lambda at, v: p_snd.__setitem__((lax.rem(s, 2),) + at, v))

                @pl.when(s >= n)
                def _():
                    copy(s - n).wait_recv()
                    tile(lambda at, v: p_rcv.__setitem__((s - n,) + at, v + p_rcv[(s - n,) + at]))
                    store(name, s - n, place(s - n), rows).start()

                @pl.when(s == 2 * n - 1)
                def _():
                    copy(n - 2).wait_send()
                    copy(n - 1).wait_send()

            def store(name, i, chip, rows):
                p = parts[name][0]
                return pltpu.make_async_copy(p_rcv.at[i, pl.ds(0, rows)], p.at[chip], pair_send.at[3 * n_chips + i])

            def stored(name, i):
                store(name, i, tile_order[i], parts[name][3]).wait()

            def pair_begin(first):
                if not first:
                    pl.semaphore_signal(pair_ready, inc=1, device_id={'tp': net.peer(0, 1)}, device_id_type=pl.DeviceIdType.MESH)
                    pl.semaphore_wait(pair_ready, 1)

            barrier = pltpu.get_barrier_semaphore()
            for chip in range(n_chips):
                for core in range(2):
                    if chip + core:
                        pl.semaphore_signal(barrier, inc=1, device_id={'tp': net.peer(chip, core)}, device_id_type=pl.DeviceIdType.MESH)
            pl.semaphore_wait(barrier, n_tp - 1)
            net.start('wq_a', 'wq_b', 'bias', 'x', 'load', 'own', 'x_own', 'dy_own')
            angle = lax.broadcasted_iota(jnp.int32, (seq, width), 0).astype(F32) * freq_ref[0:1, :]
            cos_t[...] = jnp.cos(angle)
            sin_t[...] = jnp.sin(angle) * freq_ref[1:2, :]
            for b in range(seqs):
                row = mask_ref[pl.ds(me * seqs + b, 1), :].astype(F32)
                ok[b] = jnp.broadcast_to(row, (LANES, seq)).T
            net.done('load')
            net.start('store')
            net.got('wq_a')
            net.start('wq_relay', 'wo_a', 'wo_b', 'wu_a', 'wu_b')
            net.got('wq_b')
            net.start('wq_fwd')
            net.done('own', 'x_own', 'dy_own')
            net.got('bias')
            for n in range(n_tp):
                b = b_all[n]
                b_att[n] = jnp.concatenate([b[i // heads, i % heads:i % heads + 1, :] for i in range(3 * heads)], axis=1)
                b_ffn[n] = u_all[n]
            net.got('x')

            def ln1(rows):
                x_hat, _ = ln_stats(x[rows, :].astype(F32))
                h1[rows, :] = (x_hat * gain1 + bias1).astype(BF16)

            loop_rows(tok, chunk, ln1)
            net.done('store')
            net.got('wq_relay')
            net.start('wq_last')
            net.got('wq_fwd', 'wq_last')

            def qkv_step(ps, w, q_ref, k_ref, v_ref):
                s = ps.index[0]
                hooks(s, {2: lambda: (net.got('wo_a'), net.start('wo_relay', 'dy')), 7: lambda: (net.got('wu_a'), net.start('wu_relay'))})
                n_src = tok // chunk // 2

                @pl.loop(0, 2)
                def _(i):
                    rows = span(i, tok // 2)
                    t = mm(h1[rows, :], w[0], NT) + b_att[s]
                    cos, sin = (t_ref[span(i, seq // 2), :].reshape(n_src, 1, p_len, width) for t_ref in (cos_t, sin_t))

                    def rope(v):
                        out = v.reshape(n_src, seqs, p_len, width) * cos + swap_halves(v, hd).reshape(n_src, seqs, p_len, width) * sin
                        return out.astype(BF16)

                    src = span(i, n_src)
                    q_ref[0, src] = rope(t[:, :width] * q_scale)
                    k_ref[0, src] = rope(t[:, width:2 * width])
                    v_ref[0, src] = t[:, 2 * width:].reshape(n_src, seqs, p_len, width).astype(BF16)

            slot3 = lambda rows, cols, f=lambda s: s: pl.BlockSpec((1, rows, cols), lambda s: (f(s), 0, 0))
            pipe = functools.partial(pltpu.emit_pipeline, _explicit_indices=True)
            pipe(qkv_step, grid=(n_tp,), in_specs=[slot3(n3, dim)], out_specs=[pl.BlockSpec((1, n_tp, seqs, p_len, width), lambda s: (s, 0, 0, 0, 0))] * 3)(
                wq, q_hbm, k_hbm, v_hbm)

            srcs = qc // p_len
            lane = lax.broadcasted_iota(jnp.int32, (qc, width), 1)

            def attn_step(ps, q_ref, k_ref, v_ref):
                g, b = ps.index
                hooks(g * seqs + b, {
                    0: lambda: (net.got('wo_b'), net.start('wo_fwd')), 1: lambda: (net.got('wo_relay'), net.start('wo_last')),
                    3: lambda: (net.got('wu_b'), net.start('wu_fwd')), 5: lambda: net.start('wd_a', 'wd_b'),
                    12: lambda: (net.got('wu_relay'), net.start('wu_last'))})
                bad = ok[b][:, 0:1] <= 0
                k = k_ref[0, :, 0].reshape(seq, width)
                v_t = v_ref[0, :, 0].reshape(seq, width).T
                for c in range(seq // qc):
                    src = slice(c * srcs, (c + 1) * srcs)
                    cols = slice(c * qc, (c + 1) * qc)
                    q = q_ref[0, src, 0].reshape(qc, width)
                    outs = []
                    for h in range(heads):
                        s = jnp.where(bad, NEG_LARGE, mm(k, jnp.where(lane // hd == h, q, jnp.zeros_like(q)), NT))
                        m = jnp.max(s, axis=0, keepdims=True)
                        e = jnp.exp(s - m)
                        r = 1.0 / col_sum(e)
                        outs.append(mm(v_t[h * hd:(h + 1) * hd], (e * r).astype(BF16), NN))
                        m_st[g, b, h:h + 1, cols] = m
                        l_st[g, b, h:h + 1, cols] = r
                    o4[src, b, :, span(g, width)] = jnp.concatenate(outs, axis=0).T.astype(BF16).reshape(srcs, p_len, width)

            head_blk = pl.BlockSpec((1, n_tp, 1, p_len, width), lambda g, b: (g, 0, b, 0, 0))
            pipe(attn_step, grid=(n_tp, seqs), in_specs=[head_blk] * 3)(q_hbm, k_hbm, v_hbm)

            net.got('wo_fwd', 'wo_last')

            @pl.loop(0, tok // (2 * chunk))
            def _(i):
                rows = span(i, 2 * chunk)
                o = o4[pl.ds(2 * i, 2)].reshape(2 * chunk, n_tp * width)
                low = (x[rows, :].astype(F32) + (mm(o, wo[...].reshape(n_tp * width, dim), NN) + bias_o)).astype(BF16)
                x1[rows, :] = low
                x_hat, _ = ln_stats(low.astype(F32))
                h2[rows, :] = (x_hat * gain2 + bias2).astype(BF16)

            net.got('wu_fwd', 'wu_last', 'dy')

            def up_step(ps, w, act_ref, slope_ref):
                s = ps.index[0]
                hooks(s, {0: lambda: (net.got('wd_a'), net.start('wd_relay')), 2: lambda: (net.got('wd_b'), net.start('wd_fwd')),
                          5: lambda: (net.got('wd_relay'), net.start('wd_last'), stored('dn', 0), net.start('dn_relay')),
                          6: lambda: (stored('dn', 1), net.start('dn_next')), 7: lambda: (stored('dn', 2), net.start('dn_prev'))})

                def gelu(rows):
                    pre = mm(h2[rows, :], w[0], NN) + b_ffn[order(s)]
                    erf_term = lax.erf(pre * INV_SQRT2)
                    act_ref[rows, :] = (0.5 * pre * (1.0 + erf_term)).astype(BF16)
                    slope_ref[rows, :] = 0.5 * (1.0 + erf_term) + pre * jnp.exp(-0.5 * pre * pre) * INV_SQRT_2PI

                loop_rows(tok, half, gelu)

                def tile(put):
                    put((pl.ds(0, ffn),), mm(act_ref[...], dy[...], TN))

                pair(s, 'dn', tile, n_tile)

            cols = pl.BlockSpec((tok, ffn), lambda s: (0, order(s)))
            wu_spec, wd_spec = slot3(dim, ffn, order), slot3(ffn, dim, order)
            pair_begin(True)
            pipe(up_step, grid=(n_tp,), in_specs=[wu_spec], out_specs=[cols, cols])(wu, act_hbm, slope_hbm)

            net.got('wd_fwd', 'wd_last')
            stored('dn', 3)
            pair_begin(False)

            def mlp_step(ps, wd_s, wu_s, act_ref, slope_ref):
                s = ps.index[0]
                hooks(s, {2: lambda: (net.got('dn_relay'), net.start('dn_load')), 3: lambda: add_relayed('dn'),
                          4: lambda: (net.done('dn_store'), net.start('dn_sum')),
                          5: lambda: (stored('up', 0), net.start('up_relay')), 6: lambda: (stored('up', 1), net.start('up_next')),
                          7: lambda: (stored('up', 2), net.start('up_prev'))})

                @pl.when(s == 0)
                def _():
                    acc[...] = jnp.zeros_like(acc)
                    acc2[...] = jnp.zeros_like(acc2)

                gb[order(s)] = jnp.zeros_like(gb[0])

                def rows_step(rows):
                    d_pre = mm(dy[rows, :], wd_s[0], NT) * slope_ref[rows, :]
                    gb[order(s)] += col_sum(d_pre)
                    low = d_pre.astype(BF16)
                    dpre[rows, :] = low
                    acc[rows, :] += mm(act_ref[rows, :], wd_s[0], NN)
                    acc2[rows, :] += mm(low, wu_s[0], NT)

                loop_rows(tok, half, rows_step)

                def tile(put):
                    for i in range(2):
                        part = pl.ds(i * half, half)
                        put((pl.ds(0, ffn), part), mm(h2[:, part], dpre[...], TN))

                pair(s, 'up', tile, n_tile)

            pipe(mlp_step, grid=(n_tp,), in_specs=[wd_spec, wu_spec, cols, cols])(wd, wu, act_hbm, slope_hbm)
            vec[...] = jnp.zeros_like(vec)

            @pl.loop(0, tok // (2 * chunk))
            def _(i):
                rows = span(i, 2 * chunk)
                x1_f, dy_f, dh = x1[rows, :].astype(F32), dy[rows, :].astype(F32), acc2[rows, :]
                x1[rows, :] = (x1_f + (acc[rows, :] + bias_d)).astype(BF16)
                x_hat, inv_std = ln_stats(x1_f)
                d_x1 = dy_f + ln_grad(dh, x_hat, inv_std, gain2)
                acc2[rows, :] = d_x1
                low = d_x1.astype(BF16)
                dx1b[rows, :] = low
                d_o = mm(low, wo[...].reshape(n_tp * width, dim), NT).astype(BF16)
                do4[pl.ds(2 * i, 2)] = d_o.reshape(2, seqs, p_len, n_tp * width)
                for n, t in enumerate((d_x1, dh * x_hat, dh, dy_f)):
                    vec[2 + n:3 + n, :] += col_sum(t)

            stored('up', 3)
            pair_begin(False)

            def bwd_step(ps, q_ref, k_ref, v_ref, w):
                step = ps.index[0]
                g = order(step)
                hooks(step, {0: lambda: net.start('y', 'y_own'), 1: lambda: (net.got('up_relay'), net.start('up_load')),
                             2: lambda: add_relayed('up'), 3: lambda: (net.done('up_store'), net.start('up_sum')),
                             5: lambda: (stored('at', 0), net.start('at_relay')), 6: lambda: (stored('at', 1), net.start('at_next')),
                             7: lambda: (stored('at', 2), net.start('at_prev'))})
                b_sum = jnp.zeros((1, n3), F32)
                for b in range(seqs):
                    bad = ok[b][:, 0:1] <= 0
                    k = k_ref[0, :, b].reshape(seq, width)
                    v = v_ref[0, :, b].reshape(seq, width)
                    k_t = k.T
                    for c in range(seq // qc):
                        src = slice(c * srcs, (c + 1) * srcs)
                        at = slice(c * qc, (c + 1) * qc)
                        q = q_ref[0, src, b].reshape(qc, width)
                        d_o = do4[src, b, :, span(g, width)].reshape(qc, width)
                        dk = jnp.zeros((seq, width), F32)
                        dv = jnp.zeros((seq, width), F32)
                        dqs = []
                        for h in range(heads):
                            mine = lane // hd == h
                            q_h = jnp.where(mine, q, jnp.zeros_like(q))
                            do_h = jnp.where(mine, d_o, jnp.zeros_like(d_o))
                            s = jnp.where(bad, NEG_LARGE, mm(k, q_h, NT))
                            p = jnp.exp(s - m_st[g, b, h:h + 1, at]) * l_st[g, b, h:h + 1, at]
                            dv += mm(p.astype(BF16), do_h, NN)
                            dp = mm(v, do_h, NT)
                            ds = (p * (dp - col_sum(dp * p))).astype(BF16)
                            dk += mm(ds, q_h, NN)
                            dqs.append(mm(k_t[h * hd:(h + 1) * hd], ds, NN))
                        dq_acc[at, :] = jnp.concatenate(dqs, axis=0).T
                        dk_acc[...] = dk if c == 0 else dk_acc[...] + dk
                        dv_acc[...] = dv if c == 0 else dv_acc[...] + dv
                    cos, sin = cos_t[...], sin_t[...]
                    dq, dk, dv = dq_acc[...], dk_acc[...], dv_acc[...]
                    dq = (dq * cos - swap_halves(dq, hd) * sin) * q_scale
                    dk = dk * cos - swap_halves(dk, hd) * sin
                    for i, t in enumerate((dq, dk, dv)):
                        d4[:, b, :, i * width:(i + 1) * width] = t.astype(BF16).reshape(n_tp, p_len, width)
                    b_sum += jnp.concatenate([col_sum(t) for t in (dq, dk, dv)], axis=1)

                @pl.when(step == 0)
                def _():
                    acc[...] = jnp.zeros_like(acc)

                @pl.loop(0, 2)
                def _(i):
                    acc[span(i, half), :] += mm(d4[pl.ds(n_chips * i, n_chips)].reshape(half, n3), w[0], NN)

                def tile(put):
                    put((pl.ds(0, n3),), mm(d4[...].reshape(tok, n3), h1[...], TN))
                    put((pl.ds(n3, width),), mm(o4[:, :, :, span(g, width)].reshape(tok, width), dx1b[...], TN))
                    rest = jnp.zeros((1, dim - n3 - ffn), F32)
                    line = jnp.concatenate([b_sum, gb[g], rest], axis=1)
                    put((pl.ds(n_tile, 16),), jnp.broadcast_to(line, (16, dim)))

                pair(step, 'at', tile, n_rows)

            slot_blk = pl.BlockSpec((1, n_tp, seqs, p_len, width), lambda s: (order(s), 0, 0, 0, 0))
            pipe(bwd_step, grid=(n_tp,), in_specs=[slot_blk] * 3 + [slot3(n3, dim, order)])(
                q_hbm, k_hbm, v_hbm, wq)

            def ln1_bwd(rows):
                x_hat, inv_std = ln_stats(x[rows, :].astype(F32))
                dh = acc[rows, :]
                h1[rows, :] = (acc2[rows, :] + ln_grad(dh, x_hat, inv_std, gain1)).astype(BF16)
                vec[0:1, :] += col_sum(dh * x_hat)
                vec[1:2, :] += col_sum(dh)

            loop_rows(tok, 2 * chunk, ln1_bwd)
            stored('at', 3)
            net.start('gx', 'gx_own', 'vec')
            net.got('at_relay')
            net.start('at_load')
            add_relayed('at')
            net.done('at_store')
            net.start('at_sum')

            def total(p, r, out, n, blocks):
                def body(_, a, b, o_ref):
                    o_ref[...] = a[0] + b[0] + b[1]

                grid, a, b, o = blocks
                pipe(body, grid=grid, in_specs=[a, b], out_specs=[o])(p, r, out)

            def by_rows(n):
                return (2,), pl.BlockSpec((1, n, dim), lambda i: (0, i, 0)), pl.BlockSpec((2, n, dim), lambda i: (0, i, 0)), pl.BlockSpec((n, dim), lambda i: (i, 0))

            net.got('dn_next', 'dn_prev', 'dn_sum')
            total(p_dn, r_dn, g_down, n_tile, by_rows(n_tile // 2))
            net.got('up_next', 'up_prev', 'up_sum')
            total(p_up, r_up, g_up, n_tile, (
                (2,), pl.BlockSpec((1, n_tile, half), lambda i: (0, 0, i)), pl.BlockSpec((2, n_tile, half), lambda i: (0, 0, i)),
                pl.BlockSpec((n_tile, half), lambda i: (i, 0))))
            net.got('vec')
            summed = vec[...]
            for n in range(1, n_tp):
                summed += vec_all[n]
            g_vec[...] = summed
            net.got('at_next', 'at_prev', 'at_sum')
            total(p_at, r_at, g_att, n_rows, by_rows(n_rows // 2))
            net.got('gx', 'y')
            net.done('y_own', 'gx_own')
            for name in net.copies:
                if name not in ('load', 'store', 'own') and not name.endswith(('_own', '_load', '_store')):
                    net.sent(name)

        big = (tok, dim)
        shapes = lambda *dims, dtype=F32: sds(dims, dtype)
        halves = lambda rows: shapes(2, rows // 2, dim)
        flat = lambda t: t.reshape(tok, dim)
        inv_freq = ROPE_BASE ** (-2.0 * jnp.arange(hd // 2, dtype=F32) / hd)
        sign = jnp.concatenate([-jnp.ones_like(inv_freq), jnp.ones_like(inv_freq)])
        freq = jnp.stack([jnp.tile(inv_freq, 2 * heads), jnp.tile(sign, heads)])
        vectors = jnp.stack([ln1_gain, ln1_bias, b_out, ln2_gain, ln2_bias, b_down])
        vmem = pl.BlockSpec(memory_space=pltpu.VMEM)
        sem = lambda n: pltpu.SemaphoreType.DMA((n,))
        outs = pl.pallas_call(
            kernel, name='layer',
            out_shape=(sds(big, BF16), sds(big, BF16), shapes(n_rows, dim), shapes(dim, ffn), shapes(ffn, dim), shapes(8, dim),
                       shapes(n_tp, n3, dim, dtype=BF16), shapes(n_tp, dim, ffn, dtype=BF16), shapes(n_tp, ffn, dim, dtype=BF16))
            + (shapes(n_tp, n_tp, seqs, p_len, width, dtype=BF16),) * 3 + (shapes(tok, n_tp * ffn, dtype=BF16), shapes(tok, n_tp * ffn))
            + tuple(shapes(n_chips, n, dim) for n in (n_tile, n_tile, n_rows)) + tuple(halves(n) for n in (n_tile, n_tile, n_rows)) * 2
            + tuple(shapes(2, n, dim) for n in (n_tile, n_tile, n_rows)),
            in_specs=[ANY, ANY, vmem, ANY, ANY, ANY, ANY, ANY, ANY, vmem, vmem], out_specs=(ANY,) * 5 + (vmem,) + (ANY,) * 20,
            scratch_shapes=[pltpu.VMEM(big, BF16)] * 3 + [pltpu.VMEM((n_tp, seqs, p_len, n_tp * width), BF16)]
            + [pltpu.VMEM(big, BF16)] * 2 + [pltpu.VMEM((n_tp, width, dim), BF16), pltpu.VMEM(big, BF16),
                                             pltpu.VMEM((n_tp, seqs, p_len, n_tp * width), BF16)]
            + [pltpu.VMEM(big, F32)] * 2 + [pltpu.VMEM((n_chips, n_rows, dim), F32), pltpu.VMEM((2, n_rows, dim), F32)]
            + [pltpu.VMEM((2, n_rows // 2, dim), F32)] * 2 + [pltpu.VMEM((n_tp, seqs, p_len, n3), BF16)]
            + [pltpu.VMEM((seq, width), F32)] * 5 + [pltpu.VMEM((seqs, seq, LANES), F32)]
            + [pltpu.VMEM((n_tp, seqs, heads, seq), F32)] * 2
            + [pltpu.VMEM((n_tp, 1, n3), F32), pltpu.VMEM((n_tp, 1, ffn), F32), pltpu.VMEM((n_tp,) + b_qkv.shape, F32)]
            + [pltpu.VMEM((n_tp, 1, ffn), F32)] * 2 + [pltpu.VMEM((8, dim), F32), pltpu.VMEM((n_tp, 8, dim), F32), pltpu.VMEM((tok, ffn), BF16)]
            + [sem(128), sem(128), sem(64), sem(4 * n_chips), sem(3 * n_chips), pltpu.SemaphoreType.REGULAR],
            compiler_params=pltpu.CompilerParams(collective_id=0, has_side_effects=True, vmem_limit_bytes=VMEM_LIMIT),
        )(flat(x_in), flat(grad_y), pad_mask, w_qkv.transpose(0, 2, 3, 1).reshape(n3, dim), b_qkv, w_out.reshape(width, dim),
          w_up, b_up.reshape(1, ffn), w_down, vectors, freq)
        y_out, grad_x, att, grad_w_up, grad_w_down, vec = outs[:6]
        grad_w_qkv = att[:n3].reshape(3, heads, hd, dim).transpose(0, 3, 1, 2)
        grad_w_out = att[n3:n_tile].reshape(heads, hd, dim)
        grad_b_qkv = att[n_tile, :n3].reshape(3, heads, hd)
        grad_b_up = att[n_tile, n3:n3 + ffn]
        return (y_out.reshape(x_in.shape), grad_x.reshape(x_in.shape), vec[0], vec[1], grad_w_qkv, grad_b_qkv, grad_w_out,
                vec[2], vec[3], vec[4], grad_w_up, grad_b_up, grad_w_down, vec[5])

    return jax.shard_map(device_step, mesh=mesh, in_specs=in_specs, out_specs=out_specs, check_vma=False)
```

time: 1320 us -> 440 us (0.33)
  waiting for transfers between devices: 877 us -> 0 us
  Pallas kernels: 0 us -> 417 us
  matrix products: 301 us -> 0 us
  other arithmetic: 87.7 us -> 0.58 us
  blocking collectives: 21.7 us -> 0 us
  between operations: 15 us -> 0.67 us
    reduce_scatter x4 -> x0, waiting for transfers between devices: 585 us -> none  [the longest x1 166 us: device_step(): lax.psum_scatter(attn_part, 'tp', scatter_dimension=1, tiled=True)]
    pallas_call x0 -> x1, Pallas kernels: none -> 417 us  [device_step(): pl.pallas_call(kernel, name='layer', out_shape=(sds(big, BF16), sds(big,...]
    all_gather x4 -> x0, waiting for transfers between devices: 291 us -> none  [the longest x1 83.3 us: device_step(): lax.all_gather(h1_f.astype(jnp.bfloat16), 'tp', axis=1, tiled=True)]
    dot_general x17 -> x0, matrix products: 267 us -> none  [the longest x1 23.3 us: device_step(): jnp.einsum('bqhk,bshk->bhqs', d_attn_o, v_heads, preferred_element_type=j...]
    convert_element_type x6 -> x0, other arithmetic: 44.1 us -> none  [the longest x1 27.6 us: device_step(): (attn_probs * (d_probs - jnp.sum(d_probs * attn_probs, axis=-1, keepdims=...]
    sub x2 -> x0, matrix products: 34.1 us -> none  [device_step(): attn_probs = jax.nn.softmax(jnp.where(key_ok, scores, NEG_LARGE), axis=-1)]
    reduce_sum x8 -> x0, other arithmetic: 28.4 us -> none  [the longest x1 6.8 us: device_step(): jnp.sum(d_x1, axis=(0, 1))]
    psum x1 -> x0, blocking collectives: 21.7 us -> none  [device_step(): lax.psum(jnp.stack([jnp.sum(d_h1 * x_hat1, axis=(0, 1)), jnp.sum(d_h1, ax...]
  transfers between devices with their start and end apart: 8 -> 0, of which waited for: 8 -> 0; matrix products, arithmetic and copies ran while one was open for 9% -> 0% of each run, Pallas kernels for 0% -> 0%
where the time goes in v3:
time: 440 us; the launch traced here: 438 us
  Pallas kernels  417 us (95%)
  local copies, waits for them, and re-layouts  19.7 us (4%)
    pallas_call x1, Pallas kernels, device_step(): pl.pallas_call(kernel, name='layer', out_shape=(sds(big, BF16), sds(big,...  417 us

profile of v3, /device:TPU:113, one launch (start us, length us, event | category | flops | bytes accessed | tf_op | source)
XLA Modules:
  0.0 438.0 jit_solution(11273401107979628948)
XLA Ops:
  0.7 0.7 tile.5
  1.3 0.1 stack_tile.7
  1.4 0.1 stack_tile.6
  1.5 0.6 pad_maximum_fusion.freq_ref
  2.1 1.4 stack.30.vecs_ref
  3.5 417.1 %layer.1 = (bf16[1024,1024]{1,0:T(8,128)(2,1)}, bf16[1024,1024]{1,0:T(8,128)(2,1)}, f32[528,1024]{1,0:T(8,128)}, f32[1024,512]{1,0:T(8,128)}, f32[512,1024]{1,0:...) custom-call(bf16[1024,1024]{1,0:T(8,128)(2,1)} %bitcast.28, ...), custom_call_target="tpu_custom_call" | custom-call | tf_op jit(solution)/shard_map/layer/pallas_call | solution.py:592
  420.6 1.3 slice.38
  421.9 0.7 slice_reduce_fusion
  422.6 0.7 reshape_squeeze.3
  423.3 1.6 fusion
  424.9 0.0 copy-start.3
  424.9 2.0 slice.34
  426.9 2.7 slice.32
  429.7 0.0 copy-done.3
  429.7 0.0 copy-start.2
  429.7 1.3 copy.33
  431.0 1.0 copy-done.2
  432.0 0.0 copy-start.1
  432.0 1.3 copy.34
  433.3 1.0 copy-done.1
  434.4 0.0 copy-start
  434.4 1.3 copy.35
  435.7 1.0 copy-done
  436.7 1.3 copy.36
  (2 shorter events, 0.0 us)
Async XLA Ops:
  424.9 4.8 %copy-start.3 = (bf16[1024,1024]{1,0:T(8,128)(2,1)S(1)}, bf16[1024,1024]{1,0:T(8,128)(2,1)}, u32[]{:S(2)}) copy-start(bf16[1024,1024]{1,0:T(8,128)(2,1)} %get-tuple-element.20) | copy-start | bytes 6291460
  429.7 2.3 copy-start.2
  432.0 2.3 copy-start.1
  434.4 2.3 copy-start

commit v4 on v3

--- a/solution.py
+++ b/solution.py
@@ -2,6 +2,7 @@
 
 import jax
 import jax.numpy as jnp
+import numpy as np
 from jax import lax
 from jax.experimental import pallas as pl
 from jax.experimental.pallas import tpu as pltpu
@@ -90,8 +91,9 @@
 
     def got(self, *names):
         for name in names:
-            for make in self.copies[name]:
-                make().wait_recv()
+            with jax.named_scope('got_' + name):
+                for make in self.copies[name]:
+                    make().wait_recv()
 
     def sent(self, *names):
         for name in names:
@@ -100,8 +102,9 @@
 
     def done(self, *names):
         for name in names:
-            for make in self.copies[name]:
-                make().wait()
+            with jax.named_scope('done_' + name):
+                for make in self.copies[name]:
+                    make().wait()
 
     def gather(self, name, own, buf):
         rows = own.shape[0]
@@ -130,15 +133,15 @@
                     self.add(name, lambda c=chip, k=core: src.at[span(self.peer(c, k), rows)], lambda: dst.at[span(me, rows)], chip, core)
         self.add_local(name + '_own', lambda: src.at[span(me, rows)], lambda: dst.at[span(me, rows)])
 
-    def scatter(self, name, p, got, summed, out):
+    def scatter(self, name, p, got, summed, early, last):
         half = p.shape[1] // 2
         top, bot = pl.ds(0, half), pl.ds(half, half)
         self.add(name + '_relay', lambda: p.at[2, top], lambda: got.at[0], 1)
         self.add(name + '_relay', lambda: p.at[2, bot], lambda: got.at[1], 3)
-        self.add(name + '_next', lambda: p.at[1, bot], lambda: out.at[0, bot], 1)
-        self.add(name + '_prev', lambda: p.at[3, top], lambda: out.at[1, top], 3)
-        self.add(name + '_sum', lambda: summed.at[0], lambda: out.at[0, top], 1)
-        self.add(name + '_sum', lambda: summed.at[1], lambda: out.at[1, bot], 3)
+        self.add(name + '_next', lambda: p.at[1, bot], lambda: early.at[bot], 1)
+        self.add(name + '_prev', lambda: p.at[3, top], lambda: early.at[top], 3)
+        self.add(name + '_sum', lambda: summed.at[0], lambda: last.at[top], 1)
+        self.add(name + '_sum', lambda: summed.at[1], lambda: last.at[bot], 3)
 
 
 def solution(mesh):
@@ -167,19 +170,21 @@
         q_scale = hd ** -0.5
         sds = jax.ShapeDtypeStruct
         n_tile = n3 + width
-        n_rows = n_tile + 16
         half = dim // 2
 
-        def kernel(x_ref, dy_ref, mask_ref, wq_ref, bq_ref, wo_ref, wu_ref, bu_ref, wd_ref, vecs_ref, freq_ref,
-                   y_out, gx_out, g_att, g_up, g_down, g_vec,
-                   wq, wu, wd, q_hbm, k_hbm, v_hbm, act_hbm, slope_hbm, p_dn, p_up, p_at, got_dn, got_up, got_at,
-                   sum_dn, sum_up, sum_at, r_dn, r_up, r_at,
-                   x, h1, dy, o4, x1, h2, wo, dx1b, do4, acc, acc2, p_rcv, p_snd, t_got, t_own, d4, dq_acc, dk_acc, dv_acc,
-                   cos_t, sin_t, ok, m_st, l_st, b_att, b_ffn, b_all, u_all, gb, vec, vec_all, dpre,
-                   send, recv, local, pair_send, pair_recv, pair_ready):
+        def kernel(*refs):
+            it = iter(refs)
+            take = lambda n: [next(it) for _ in range(n)]
+            (x_ref, dy_ref, wq_ref, bq_ref, wo_ref, wu_ref, bu_ref, wd_ref), plain = take(8), take(8)
+            y_out, gx_out, g_up, g_down, g_at, g_vec, g_b, wq, wu, wd, q_hbm, k_hbm, v_hbm, act_hbm, slope_hbm = take(15)
+            parts = {name: take(5) for name in ('dn', 'up', 'at')}
+            x, h1, dy, x1, h2, dx1b, o4, do4, wo, acc, acc2, p_rcv, p_snd, t_got, t_own, d4 = take(16)
+            dq_acc, dk_acc, dv_acc, cos_t, sin_t, ok, m_st, l_st, b_att, b_ffn, u_all, gb, b_all, b8, b_in, vec, v_in, v_sum, v_all, dpre = take(20)
+            here = take(8)
+            send, recv, local, pair_send, pair_recv, pair_ready = take(6)
             net = Net(n_tp, send, recv, local)
             me = lax.axis_index('tp')
-            gain1, bias1, bias_o, gain2, bias2, bias_d = (vecs_ref[i:i + 1, :] for i in range(6))
+            mask_ref, gain1, bias1, bias_o, gain2, bias_d, bias2, freq_ref = here
 
             net.gather('wq', wq_ref, wq)
             net.gather('wo', wo_ref, wo)
@@ -195,10 +200,14 @@
                         slot = 2 * (-chip % n_chips) + core
                         net.add('bias', lambda: bq_ref, lambda n=slot: b_all.at[n], chip, core)
                         net.add('bias', lambda: bu_ref, lambda n=slot: u_all.at[n], chip, core)
-                        net.add('vec', lambda: vec, lambda n=slot: vec_all.at[n], chip, core)
-            net.scatter('dn', p_dn, got_dn, sum_dn, r_dn)
-            net.scatter('up', p_up, got_up, sum_up, r_up)
-            net.scatter('at', p_at, got_at, sum_at, r_at)
+                        own = 2 * chip + core
+                        net.add('b8', lambda n=own: b8.at[n], lambda n=slot: b_in.at[n], chip, core)
+                        net.add('vec', lambda c=chip, k=core: vec.at[:, span(net.peer(c, k), LANES)], lambda n=slot: v_in.at[n], chip, core)
+                        net.add('v_sum', lambda: v_sum, lambda: v_all.at[:, span(me, LANES)], chip, core)
+            for src, dst in zip(plain, here):
+                net.add_local('own', lambda r=src: r, lambda r=dst: r)
+            net.add_local('write', lambda: v_all, lambda: g_vec)
+            net.add_local('write', lambda: b8.at[0], lambda: g_b)
             for name, ref, tmp, buf in (('wq', wq_ref, lambda: h2.at[pl.ds(0, n3)], wq), ('wu', wu_ref, lambda: x1.at[:, pl.ds(0, ffn)], wu),
                                         ('wd', wd_ref, lambda: dx1b.at[pl.ds(0, ffn)], wd)):
                 net.add_local('load', lambda r=ref: r, tmp)
@@ -206,23 +215,22 @@
             net.add_local('own', lambda: wo_ref, lambda: wo.at[0])
             net.add_local('own', lambda: bq_ref, lambda: b_all.at[0])
             net.add_local('own', lambda: bu_ref, lambda: u_all.at[0])
-            parts = {'dn': (p_dn, got_dn, sum_dn, n_tile), 'up': (p_up, got_up, sum_up, n_tile), 'at': (p_at, got_at, sum_at, n_rows)}
-            for name, (p, got, summed, rows) in parts.items():
-                h = rows // 2
-                for i, (j, lo) in enumerate(((1, 0), (3, h))):
-                    net.add_local(name + '_load', lambda g=got, i=i: g.at[i], lambda i=i, h=h: t_got.at[i, pl.ds(0, h)])
-                    net.add_local(name + '_load', lambda p=p, j=j, lo=lo, h=h: p.at[j, pl.ds(lo, h)], lambda i=i, h=h: t_own.at[i, pl.ds(0, h)])
-                    net.add_local(name + '_store', lambda i=i, h=h: t_own.at[i, pl.ds(0, h)], lambda s=summed, i=i: s.at[i])
+            t_half = n_tile // 2
+            for name, (p, got, summed, early, last) in parts.items():
+                net.scatter(name, p, got, summed, early, last)
+                for i in range(2):
+                    net.add_local(name + '_load', lambda g=got, i=i: g.at[i], lambda i=i: t_got.at[i])
+                    net.add_local(name + '_load', lambda p=p, i=i: p.at[1 + 2 * i, pl.ds(i * t_half, t_half)], lambda i=i: t_own.at[i])
+                    net.add_local(name + '_store', lambda i=i: t_own.at[i], lambda s=summed, i=i: s.at[i])
 
             def add_relayed(name):
-                h = parts[name][3] // 2
                 net.done(name + '_load')
 
                 def body(rows):
                     for i in range(2):
                         t_own[i, rows] += t_got[i, rows]
 
-                loop_rows(h, 8, body)
+                loop_rows(t_half, 8, body)
                 net.start(name + '_store')
 
             def hooks(step, table):
@@ -239,14 +247,13 @@
             def order(s):
                 return 2 * place(lax.rem(s, n_chips)) + 1 - lax.div(s, n_chips)
 
-            def pair(s, name, tile, rows):
+            def pair(s, name, tile):
                 n = n_chips
                 base = n * list(parts).index(name)
-                p = parts[name][0]
 
                 def copy(i):
                     return pltpu.make_async_remote_copy(
-                        src_ref=p_snd.at[lax.rem(i, 2), pl.ds(0, rows)], dst_ref=p_rcv.at[i, pl.ds(0, rows)],
+                        src_ref=p_snd.at[lax.rem(i, 2)], dst_ref=p_rcv.at[i],
                         send_sem=pair_send.at[base + i], recv_sem=pair_recv.at[base + i],
                         device_id={'tp': net.peer(0, 1)}, device_id_type=pl.DeviceIdType.MESH)
 
@@ -266,19 +273,18 @@
                 def _():
                     copy(s - n).wait_recv()
                     tile(lambda at, v: p_rcv.__setitem__((s - n,) + at, v + p_rcv[(s - n,) + at]))
-                    store(name, s - n, place(s - n), rows).start()
+                    store(name, s - n, place(s - n)).start()
 
                 @pl.when(s == 2 * n - 1)
                 def _():
                     copy(n - 2).wait_send()
                     copy(n - 1).wait_send()
 
-            def store(name, i, chip, rows):
-                p = parts[name][0]
-                return pltpu.make_async_copy(p_rcv.at[i, pl.ds(0, rows)], p.at[chip], pair_send.at[3 * n_chips + i])
+            def store(name, i, chip):
+                return pltpu.make_async_copy(p_rcv.at[i], parts[name][0].at[chip], pair_send.at[3 * n_chips + i])
 
             def stored(name, i):
-                store(name, i, tile_order[i], parts[name][3]).wait()
+                store(name, i, tile_order[i]).wait()
 
             def pair_begin(first):
                 if not first:
@@ -291,7 +297,8 @@
                     if chip + core:
                         pl.semaphore_signal(barrier, inc=1, device_id={'tp': net.peer(chip, core)}, device_id_type=pl.DeviceIdType.MESH)
             pl.semaphore_wait(barrier, n_tp - 1)
-            net.start('wq_a', 'wq_b', 'bias', 'x', 'load', 'own', 'x_own', 'dy_own')
+            net.start('wq_a', 'wq_b', 'bias', 'x', 'own', 'load', 'x_own', 'dy_own')
+            net.done('own')
             angle = lax.broadcasted_iota(jnp.int32, (seq, width), 0).astype(F32) * freq_ref[0:1, :]
             cos_t[...] = jnp.cos(angle)
             sin_t[...] = jnp.sin(angle) * freq_ref[1:2, :]
@@ -301,10 +308,10 @@
             net.done('load')
             net.start('store')
             net.got('wq_a')
-            net.start('wq_relay', 'wo_a', 'wo_b', 'wu_a', 'wu_b')
+            net.start('wq_relay', 'wo_a', 'wo_b')
             net.got('wq_b')
             net.start('wq_fwd')
-            net.done('own', 'x_own', 'dy_own')
+            net.done('x_own', 'dy_own')
             net.got('bias')
             for n in range(n_tp):
                 b = b_all[n]
@@ -314,7 +321,7 @@
 
             def ln1(rows):
                 x_hat, _ = ln_stats(x[rows, :].astype(F32))
-                h1[rows, :] = (x_hat * gain1 + bias1).astype(BF16)
+                h1[rows, :] = (x_hat * gain1[...] + bias1[...]).astype(BF16)
 
             loop_rows(tok, chunk, ln1)
             net.done('store')
@@ -324,7 +331,8 @@
 
             def qkv_step(ps, w, q_ref, k_ref, v_ref):
                 s = ps.index[0]
-                hooks(s, {2: lambda: (net.got('wo_a'), net.start('wo_relay', 'dy')), 7: lambda: (net.got('wu_a'), net.start('wu_relay'))})
+                hooks(s, {1: lambda: (net.got('wo_a'), net.start('wo_relay', 'wu_a', 'wu_b')), 3: lambda: (net.got('wo_b'), net.start('wo_fwd')),
+                          5: lambda: (net.got('wo_relay'), net.start('wo_last'))})
                 n_src = tok // chunk // 2
 
                 @pl.loop(0, 2)
@@ -343,7 +351,14 @@
                     v_ref[0, src] = t[:, 2 * width:].reshape(n_src, seqs, p_len, width).astype(BF16)
 
             slot3 = lambda rows, cols, f=lambda s: s: pl.BlockSpec((1, rows, cols), lambda s: (f(s), 0, 0))
-            pipe = functools.partial(pltpu.emit_pipeline, _explicit_indices=True)
+
+            def pipe(body, **specs):
+                def run(*refs):
+                    with jax.named_scope(body.__name__):
+                        pltpu.emit_pipeline(body, _explicit_indices=True, **specs)(*refs)
+
+                return run
+
             pipe(qkv_step, grid=(n_tp,), in_specs=[slot3(n3, dim)], out_specs=[pl.BlockSpec((1, n_tp, seqs, p_len, width), lambda s: (s, 0, 0, 0, 0))] * 3)(
                 wq, q_hbm, k_hbm, v_hbm)
 
@@ -353,9 +368,8 @@
             def attn_step(ps, q_ref, k_ref, v_ref):
                 g, b = ps.index
                 hooks(g * seqs + b, {
-                    0: lambda: (net.got('wo_b'), net.start('wo_fwd')), 1: lambda: (net.got('wo_relay'), net.start('wo_last')),
-                    3: lambda: (net.got('wu_b'), net.start('wu_fwd')), 5: lambda: net.start('wd_a', 'wd_b'),
-                    12: lambda: (net.got('wu_relay'), net.start('wu_last'))})
+                    0: lambda: (net.got('wu_a'), net.start('wu_relay', 'dy')), 6: lambda: (net.got('wu_b'), net.start('wu_fwd')),
+                    11: lambda: (net.got('wu_relay'), net.start('wu_last', 'wd_a', 'wd_b'))})
                 bad = ok[b][:, 0:1] <= 0
                 k = k_ref[0, :, 0].reshape(seq, width)
                 v_t = v_ref[0, :, 0].reshape(seq, width).T
@@ -383,18 +397,17 @@
             def _(i):
                 rows = span(i, 2 * chunk)
                 o = o4[pl.ds(2 * i, 2)].reshape(2 * chunk, n_tp * width)
-                low = (x[rows, :].astype(F32) + (mm(o, wo[...].reshape(n_tp * width, dim), NN) + bias_o)).astype(BF16)
+                low = (x[rows, :].astype(F32) + (mm(o, wo[...].reshape(n_tp * width, dim), NN) + bias_o[...])).astype(BF16)
                 x1[rows, :] = low
                 x_hat, _ = ln_stats(low.astype(F32))
-                h2[rows, :] = (x_hat * gain2 + bias2).astype(BF16)
+                h2[rows, :] = (x_hat * gain2[...] + bias2[...]).astype(BF16)
 
             net.got('wu_fwd', 'wu_last', 'dy')
 
             def up_step(ps, w, act_ref, slope_ref):
                 s = ps.index[0]
-                hooks(s, {0: lambda: (net.got('wd_a'), net.start('wd_relay')), 2: lambda: (net.got('wd_b'), net.start('wd_fwd')),
-                          5: lambda: (net.got('wd_relay'), net.start('wd_last'), stored('dn', 0), net.start('dn_relay')),
-                          6: lambda: (stored('dn', 1), net.start('dn_next')), 7: lambda: (stored('dn', 2), net.start('dn_prev'))})
+                hooks(s, {3: lambda: (net.got('wd_a'), net.start('wd_relay')), 5: lambda: (stored('dn', 0), net.start('dn_relay')),
+                          6: lambda: (stored('dn', 1), net.start('dn_next')), 7: lambda: (stored('dn', 2), net.start('dn_prev'), net.got('wd_b'), net.start('wd_fwd'))})
 
                 def gelu(rows):
                     pre = mm(h2[rows, :], w[0], NN) + b_ffn[order(s)]
@@ -407,22 +420,24 @@
                 def tile(put):
                     put((pl.ds(0, ffn),), mm(act_ref[...], dy[...], TN))
 
-                pair(s, 'dn', tile, n_tile)
+                pair(s, 'dn', tile)
 
             cols = pl.BlockSpec((tok, ffn), lambda s: (0, order(s)))
             wu_spec, wd_spec = slot3(dim, ffn, order), slot3(ffn, dim, order)
             pair_begin(True)
             pipe(up_step, grid=(n_tp,), in_specs=[wu_spec], out_specs=[cols, cols])(wu, act_hbm, slope_hbm)
 
+            net.got('wd_relay')
+            net.start('wd_last')
             net.got('wd_fwd', 'wd_last')
             stored('dn', 3)
             pair_begin(False)
 
             def mlp_step(ps, wd_s, wu_s, act_ref, slope_ref):
                 s = ps.index[0]
-                hooks(s, {2: lambda: (net.got('dn_relay'), net.start('dn_load')), 3: lambda: add_relayed('dn'),
-                          4: lambda: (net.done('dn_store'), net.start('dn_sum')),
-                          5: lambda: (stored('up', 0), net.start('up_relay')), 6: lambda: (stored('up', 1), net.start('up_next')),
+                hooks(s, {4: lambda: (net.got('dn_relay'), net.start('dn_load')),
+                          5: lambda: (add_relayed('dn'), stored('up', 0), net.start('up_relay')),
+                          6: lambda: (net.done('dn_store'), net.start('dn_sum'), stored('up', 1), net.start('up_next')),
                           7: lambda: (stored('up', 2), net.start('up_prev'))})
 
                 @pl.when(s == 0)
@@ -447,7 +462,7 @@
                         part = pl.ds(i * half, half)
                         put((pl.ds(0, ffn), part), mm(h2[:, part], dpre[...], TN))
 
-                pair(s, 'up', tile, n_tile)
+                pair(s, 'up', tile)
 
             pipe(mlp_step, grid=(n_tp,), in_specs=[wd_spec, wu_spec, cols, cols])(wd, wu, act_hbm, slope_hbm)
             vec[...] = jnp.zeros_like(vec)
@@ -456,9 +471,9 @@
             def _(i):
                 rows = span(i, 2 * chunk)
                 x1_f, dy_f, dh = x1[rows, :].astype(F32), dy[rows, :].astype(F32), acc2[rows, :]
-                x1[rows, :] = (x1_f + (acc[rows, :] + bias_d)).astype(BF16)
+                x1[rows, :] = (x1_f + (acc[rows, :] + bias_d[...])).astype(BF16)
                 x_hat, inv_std = ln_stats(x1_f)
-                d_x1 = dy_f + ln_grad(dh, x_hat, inv_std, gain2)
+                d_x1 = dy_f + ln_grad(dh, x_hat, inv_std, gain2[...])
                 acc2[rows, :] = d_x1
                 low = d_x1.astype(BF16)
                 dx1b[rows, :] = low
@@ -473,11 +488,13 @@
             def bwd_step(ps, q_ref, k_ref, v_ref, w):
                 step = ps.index[0]
                 g = order(step)
-                hooks(step, {0: lambda: net.start('y', 'y_own'), 1: lambda: (net.got('up_relay'), net.start('up_load')),
-                             2: lambda: add_relayed('up'), 3: lambda: (net.done('up_store'), net.start('up_sum')),
-                             5: lambda: (stored('at', 0), net.start('at_relay')), 6: lambda: (stored('at', 1), net.start('at_next')),
+                hooks(step, {0: lambda: net.start('y', 'y_own'), 4: lambda: (net.got('up_relay'), net.start('up_load')),
+                             5: lambda: (add_relayed('up'), stored('at', 0), net.start('at_relay')),
+                             6: lambda: (net.done('up_store'), net.start('up_sum'), stored('at', 1), net.start('at_next')),
                              7: lambda: (stored('at', 2), net.start('at_prev'))})
-                b_sum = jnp.zeros((1, n3), F32)
+                b8[g] = jnp.zeros_like(b8[0])
+                for i in range(ffn // LANES):
+                    b8[g, 3 + i:4 + i, :] = gb[g][:, i * LANES:(i + 1) * LANES]
                 for b in range(seqs):
                     bad = ok[b][:, 0:1] <= 0
                     k = k_ref[0, :, b].reshape(seq, width)
@@ -511,7 +528,7 @@
                     dk = dk * cos - swap_halves(dk, hd) * sin
                     for i, t in enumerate((dq, dk, dv)):
                         d4[:, b, :, i * width:(i + 1) * width] = t.astype(BF16).reshape(n_tp, p_len, width)
-                    b_sum += jnp.concatenate([col_sum(t) for t in (dq, dk, dv)], axis=1)
+                        b8[g, i:i + 1, :] += col_sum(t)
 
                 @pl.when(step == 0)
                 def _():
@@ -524,11 +541,8 @@
                 def tile(put):
                     put((pl.ds(0, n3),), mm(d4[...].reshape(tok, n3), h1[...], TN))
                     put((pl.ds(n3, width),), mm(o4[:, :, :, span(g, width)].reshape(tok, width), dx1b[...], TN))
-                    rest = jnp.zeros((1, dim - n3 - ffn), F32)
-                    line = jnp.concatenate([b_sum, gb[g], rest], axis=1)
-                    put((pl.ds(n_tile, 16),), jnp.broadcast_to(line, (16, dim)))
-
-                pair(step, 'at', tile, n_rows)
+
+                pair(step, 'at', tile)
 
             slot_blk = pl.BlockSpec((1, n_tp, seqs, p_len, width), lambda s: (order(s), 0, 0, 0, 0))
             pipe(bwd_step, grid=(n_tp,), in_specs=[slot_blk] * 3 + [slot3(n3, dim, order)])(
@@ -537,85 +551,121 @@
             def ln1_bwd(rows):
                 x_hat, inv_std = ln_stats(x[rows, :].astype(F32))
                 dh = acc[rows, :]
-                h1[rows, :] = (acc2[rows, :] + ln_grad(dh, x_hat, inv_std, gain1)).astype(BF16)
+                h1[rows, :] = (acc2[rows, :] + ln_grad(dh, x_hat, inv_std, gain1[...])).astype(BF16)
                 vec[0:1, :] += col_sum(dh * x_hat)
                 vec[1:2, :] += col_sum(dh)
 
             loop_rows(tok, 2 * chunk, ln1_bwd)
             stored('at', 3)
-            net.start('gx', 'gx_own', 'vec')
+            net.start('b8', 'vec', 'gx', 'gx_own')
+
+            def total(name, out, n_in, block, at):
+                def body(*blocks):
+                    p_blk, more, o_blk = blocks[1], blocks[2:-1], blocks[-1]
+                    v = p_blk[0]
+                    for m in more:
+                        v += m[...]
+                    o_blk[...] = v
+
+                p, _, _, early, last = parts[name]
+                pipe(body, grid=(2,), in_specs=[pl.BlockSpec((1,) + block, lambda i: (0,) + at(i))] + [pl.BlockSpec(block, at)] * n_in,
+                     out_specs=[pl.BlockSpec(block, lambda i: (i, 0))])(p, *(early, last)[:n_in], out)
+
+            by_row, by_col = lambda i: (i, 0), lambda i: (0, i)
+            net.got('dn_next', 'dn_prev', 'dn_sum')
+            total('dn', g_down, 2, (t_half, dim), by_row)
+            net.got('b8', 'vec')
+            b_total, v_total = b8[0], vec[:, span(me, LANES)]
+            for n in range(1, n_tp):
+                b_total += b_in[n]
+                v_total += v_in[n]
+            b8[0] = b_total
+            v_sum[...] = v_total
+            v_all[:, span(me, LANES)] = v_total
             net.got('at_relay')
             net.start('at_load')
             add_relayed('at')
             net.done('at_store')
-            net.start('at_sum')
-
-            def total(p, r, out, n, blocks):
-                def body(_, a, b, o_ref):
-                    o_ref[...] = a[0] + b[0] + b[1]
-
-                grid, a, b, o = blocks
-                pipe(body, grid=grid, in_specs=[a, b], out_specs=[o])(p, r, out)
-
-            def by_rows(n):
-                return (2,), pl.BlockSpec((1, n, dim), lambda i: (0, i, 0)), pl.BlockSpec((2, n, dim), lambda i: (0, i, 0)), pl.BlockSpec((n, dim), lambda i: (i, 0))
-
-            net.got('dn_next', 'dn_prev', 'dn_sum')
-            total(p_dn, r_dn, g_down, n_tile, by_rows(n_tile // 2))
+            net.start('v_sum', 'at_sum')
             net.got('up_next', 'up_prev', 'up_sum')
-            total(p_up, r_up, g_up, n_tile, (
-                (2,), pl.BlockSpec((1, n_tile, half), lambda i: (0, 0, i)), pl.BlockSpec((2, n_tile, half), lambda i: (0, 0, i)),
-                pl.BlockSpec((n_tile, half), lambda i: (i, 0))))
-            net.got('vec')
-            summed = vec[...]
-            for n in range(1, n_tp):
-                summed += vec_all[n]
-            g_vec[...] = summed
-            net.got('at_next', 'at_prev', 'at_sum')
-            total(p_at, r_at, g_att, n_rows, by_rows(n_rows // 2))
-            net.got('gx', 'y')
-            net.done('y_own', 'gx_own')
+            total('up', g_up, 2, (n_tile, half), by_col)
+            net.got('at_next', 'at_prev')
+            total('at', g_at, 1, (t_half, dim), by_row)
+            late = ('gx', 'v_sum', 'at_sum')
+            local_ends = ('_own', '_load', '_store')
             for name in net.copies:
-                if name not in ('load', 'store', 'own') and not name.endswith(('_own', '_load', '_store')):
+                if name not in ('load', 'store', 'own', 'write') + late and not name.endswith(local_ends):
                     net.sent(name)
+            net.got('gx', 'y', 'v_sum')
+            net.start('write')
+            net.done('y_own', 'gx_own', 'write')
+            net.sent('gx', 'v_sum')
+            net.got('at_sum')
+            net.sent('at_sum')
 
         big = (tok, dim)
         shapes = lambda *dims, dtype=F32: sds(dims, dtype)
-        halves = lambda rows: shapes(2, rows // 2, dim)
         flat = lambda t: t.reshape(tok, dim)
-        inv_freq = ROPE_BASE ** (-2.0 * jnp.arange(hd // 2, dtype=F32) / hd)
-        sign = jnp.concatenate([-jnp.ones_like(inv_freq), jnp.ones_like(inv_freq)])
-        freq = jnp.stack([jnp.tile(inv_freq, 2 * heads), jnp.tile(sign, heads)])
-        vectors = jnp.stack([ln1_gain, ln1_bias, b_out, ln2_gain, ln2_bias, b_down])
-        vmem = pl.BlockSpec(memory_space=pltpu.VMEM)
+        inv_freq = ROPE_BASE ** (-2.0 * np.arange(hd // 2) / hd)
+        sign = np.repeat([-1.0, 1.0], hd // 2)
+        freq = np.stack([np.tile(inv_freq, 2 * heads), np.tile(sign, heads)]).astype(np.float32)
+        line = lambda v: v.reshape(1, -1)
         sem = lambda n: pltpu.SemaphoreType.DMA((n,))
+        low = functools.partial(shapes, dtype=BF16)
+        weights = [low(n_tp, n3, dim), low(n_tp, dim, ffn), low(n_tp, ffn, dim)]
+        reduction = [shapes(n_chips, n_tile, dim), shapes(2, n_tile // 2, dim), shapes(2, n_tile // 2, dim), shapes(n_tile, dim), shapes(n_tile, dim)]
+        out_shape = ([low(*big)] * 2 + [shapes(dim, ffn), shapes(ffn, dim), shapes(n_tile, dim), shapes(8, dim), shapes(8, LANES)] + weights
+                     + [low(n_tp, n_tp, seqs, p_len, width)] * 3 + [low(tok, n_tp * ffn), shapes(tok, n_tp * ffn)] + reduction * 3)
+        plain = [pad_mask] + [line(v) for v in (ln1_gain, ln1_bias, b_out, ln2_gain, b_down, ln2_bias)] + [freq]
+        heads4 = low(n_tp, seqs, p_len, n_tp * width)
+        stat = shapes(n_tp, seqs, heads, seq)
+        tile8 = shapes(n_tp, 8, LANES)
+        row_ffn = shapes(n_tp, 1, ffn)
+        scratch = ([low(*big)] * 6 + [heads4, heads4, low(n_tp, width, dim)] + [shapes(*big)] * 2
+                   + [shapes(n_chips, n_tile, dim)] + [shapes(2, n_tile, dim)] + [shapes(2, n_tile // 2, dim)] * 2 + [low(n_tp, seqs, p_len, n3)]
+                   + [shapes(seq, width)] * 5 + [shapes(seqs, seq, LANES), stat, stat, shapes(n_tp, 1, n3), row_ffn, row_ffn, row_ffn]
+                   + [shapes(n_tp, *b_qkv.shape), tile8, tile8, shapes(8, dim), tile8, shapes(8, LANES), shapes(8, dim), low(tok, ffn)] + plain)
         outs = pl.pallas_call(
-            kernel, name='layer',
-            out_shape=(sds(big, BF16), sds(big, BF16), shapes(n_rows, dim), shapes(dim, ffn), shapes(ffn, dim), shapes(8, dim),
-                       shapes(n_tp, n3, dim, dtype=BF16), shapes(n_tp, dim, ffn, dtype=BF16), shapes(n_tp, ffn, dim, dtype=BF16))
-            + (shapes(n_tp, n_tp, seqs, p_len, width, dtype=BF16),) * 3 + (shapes(tok, n_tp * ffn, dtype=BF16), shapes(tok, n_tp * ffn))
-            + tuple(shapes(n_chips, n, dim) for n in (n_tile, n_tile, n_rows)) + tuple(halves(n) for n in (n_tile, n_tile, n_rows)) * 2
-            + tuple(shapes(2, n, dim) for n in (n_tile, n_tile, n_rows)),
-            in_specs=[ANY, ANY, vmem, ANY, ANY, ANY, ANY, ANY, ANY, vmem, vmem], out_specs=(ANY,) * 5 + (vmem,) + (ANY,) * 20,
-            scratch_shapes=[pltpu.VMEM(big, BF16)] * 3 + [pltpu.VMEM((n_tp, seqs, p_len, n_tp * width), BF16)]
-            + [pltpu.VMEM(big, BF16)] * 2 + [pltpu.VMEM((n_tp, width, dim), BF16), pltpu.VMEM(big, BF16),
-                                             pltpu.VMEM((n_tp, seqs, p_len, n_tp * width), BF16)]
-            + [pltpu.VMEM(big, F32)] * 2 + [pltpu.VMEM((n_chips, n_rows, dim), F32), pltpu.VMEM((2, n_rows, dim), F32)]
-            + [pltpu.VMEM((2, n_rows // 2, dim), F32)] * 2 + [pltpu.VMEM((n_tp, seqs, p_len, n3), BF16)]
-            + [pltpu.VMEM((seq, width), F32)] * 5 + [pltpu.VMEM((seqs, seq, LANES), F32)]
-            + [pltpu.VMEM((n_tp, seqs, heads, seq), F32)] * 2
-            + [pltpu.VMEM((n_tp, 1, n3), F32), pltpu.VMEM((n_tp, 1, ffn), F32), pltpu.VMEM((n_tp,) + b_qkv.shape, F32)]
-            + [pltpu.VMEM((n_tp, 1, ffn), F32)] * 2 + [pltpu.VMEM((8, dim), F32), pltpu.VMEM((n_tp, 8, dim), F32), pltpu.VMEM((tok, ffn), BF16)]
+            kernel, name='layer', out_shape=out_shape, in_specs=[ANY] * 16, out_specs=[ANY] * len(out_shape),
+            scratch_shapes=[pltpu.VMEM(v.shape, v.dtype) for v in scratch]
             + [sem(128), sem(128), sem(64), sem(4 * n_chips), sem(3 * n_chips), pltpu.SemaphoreType.REGULAR],
             compiler_params=pltpu.CompilerParams(collective_id=0, has_side_effects=True, vmem_limit_bytes=VMEM_LIMIT),
-        )(flat(x_in), flat(grad_y), pad_mask, w_qkv.transpose(0, 2, 3, 1).reshape(n3, dim), b_qkv, w_out.reshape(width, dim),
-          w_up, b_up.reshape(1, ffn), w_down, vectors, freq)
-        y_out, grad_x, att, grad_w_up, grad_w_down, vec = outs[:6]
-        grad_w_qkv = att[:n3].reshape(3, heads, hd, dim).transpose(0, 3, 1, 2)
-        grad_w_out = att[n3:n_tile].reshape(heads, hd, dim)
-        grad_b_qkv = att[n_tile, :n3].reshape(3, heads, hd)
-        grad_b_up = att[n_tile, n3:n3 + ffn]
-        return (y_out.reshape(x_in.shape), grad_x.reshape(x_in.shape), vec[0], vec[1], grad_w_qkv, grad_b_qkv, grad_w_out,
-                vec[2], vec[3], vec[4], grad_w_up, grad_b_up, grad_w_down, vec[5])
+        )(flat(x_in), flat(grad_y), w_qkv.transpose(0, 2, 3, 1).reshape(n3, dim), b_qkv, w_out.reshape(width, dim),
+          w_up, line(b_up), w_down, *plain)
+
+        def finish(y_ref, gx_ref, gu_ref, gd_ref, v_ref, b_ref, pq, po, lq, lo, y_o, gx_o, gu_o, gd_o, gq_o, go_o, bq_o, bu_o, *v_o):
+            y_o[...], gx_o[...], gu_o[...], gd_o[...] = y_ref[...], gx_ref[...], gu_ref[...], gd_ref[...]
+            gq_o[...] = pq[...] + lq[...]
+            go_o[...] = po[...] + lo[...]
+            for i in range(3):
+                for h in range(heads):
+                    bq_o[i, h:h + 1, :] = b_ref[i:i + 1, h * hd:(h + 1) * hd]
+            for i in range(ffn // LANES):
+                bu_o[:, i * LANES:(i + 1) * LANES] = b_ref[3 + i:4 + i, :]
+            for i, ref in enumerate(v_o):
+                ref[...] = v_ref[i:i + 1, :]
+
+        n_step = 4
+
+        def cut(rows, cols, first=0):
+            return pl.BlockSpec((rows // n_step, cols), lambda i: (first * n_step // rows + i, 0))
+
+        def const(*dims):
+            return pl.BlockSpec(dims, lambda i: (0,) * len(dims))
+
+        main = [cut(tok, dim), cut(tok, dim), cut(dim, ffn), cut(ffn, dim)]
+        att = [cut(n3, dim), cut(width, dim, n3)]
+        res = pl.pallas_call(
+            finish, name='finish', grid=(n_step,),
+            out_shape=(sds(big, BF16), sds(big, BF16), shapes(dim, ffn), shapes(ffn, dim), shapes(n3, dim), shapes(width, dim),
+                       shapes(*b_qkv.shape), shapes(1, ffn)) + (shapes(1, dim),) * 6,
+            in_specs=main + [const(8, dim), const(8, LANES)] + att * 2,
+            out_specs=tuple(main) + (cut(n3, dim), cut(width, dim), const(*b_qkv.shape), const(1, ffn)) + (const(1, dim),) * 6,
+            compiler_params=pltpu.CompilerParams(vmem_limit_bytes=VMEM_LIMIT),
+        )(*outs[:4], *outs[5:7], outs[4], outs[4], outs[-1], outs[-1])
+        y_out, grad_x, grad_w_up, grad_w_down, gq, go, grad_b_qkv, grad_b_up = res[:8]
+        v = [t.reshape(dim) for t in res[8:]]
+        return (y_out.reshape(x_in.shape), grad_x.reshape(x_in.shape), v[0], v[1], gq.reshape(3, heads, hd, dim).transpose(0, 3, 1, 2),
+                grad_b_qkv, go.reshape(heads, hd, dim), v[2], v[3], v[4], grad_w_up, grad_b_up.reshape(ffn), grad_w_down, v[5])
 
     return jax.shard_map(device_step, mesh=mesh, in_specs=in_specs, out_specs=out_specs, check_vma=False)

time: 440 us -> 416 us (0.945)
  local copies, waits for them, and re-layouts: 19.7 us -> 0 us
    slice x5 -> x0, local copies, waits for them, and re-layouts: 8.4 us -> none  [the longest x1 2.73 us: device_step(): grad_w_qkv = att[:n3].reshape(3, heads, hd, dim).transpose(0, 3, 1, 2)]
    unnamed x12 -> x0, local copies, waits for them, and re-layouts: 8.36 us -> none
    pallas_call x1 -> x2, Pallas kernels: 417 us -> 415 us  [the longest x1 407 us: device_step(): pl.pallas_call(kernel, name='layer', out_shape=out_shape, in_specs=[ANY]...]
where the time goes in v4:
time: 416 us
  Pallas kernels  415 us (100%)
    pallas_call x1, Pallas kernels, device_step(): pl.pallas_call(kernel, name='layer', out_shape=out_shape, in_specs=[ANY]...  407 us

profile of v4, /device:TPU:113, one launch (start us, length us, event | category | flops | bytes accessed | tf_op | source)
XLA Modules:
  0.0 415.6 jit_solution(10845367988608829266)
XLA Ops:
  0.7 406.6 %layer.1 = (bf16[1024,1024]{1,0:T(8,128)(2,1)}, bf16[1024,1024]{1,0:T(8,128)(2,1)}, f32[1024,512]{1,0:T(8,128)}, f32[512,1024]{1,0:T(8,128)}, f32[512,1024]{1,0:...) custom-call(bf16[1024,1024]{1,0:T(8,128)(2,1)} %bitcast.26, ...), custom_call_target="tpu_custom_call" | custom-call | tf_op jit(solution)/shard_map/layer/pallas_call | solution.py:628
  407.3 8.2 %finish.1 = (bf16[1024,1024]{1,0:T(8,128)(2,1)}, bf16[1024,1024]{1,0:T(8,128)(2,1)}, f32[1024,512]{1,0:T(8,128)}, f32[512,1024]{1,0:T(8,128)}, f32[384,1024]{1,0...) custom-call(bf16[1024,1024]{1,0:T(8,128)(2,1)} %get-tuple-element.36, ...), custom_call_target="tpu_custom_call" | custom-call | tf_op jit(solution)/shard_map/finish/pallas_call | solution.py:658
